TPU v7x, 256 devices: a whole 4x4x8 slice. The times are simulated.
256 devices in a mesh: expert: 64 (over x_lo, z, y), tensor: 4 (over x_hi, core).
Axes of the slice: x: 4 (x_hi: 2, x_lo: 2; x = x_hi * 2 + x_lo), y: 4, z: 8, core: 2. Of those that a mesh axis runs over, the one named last changes fastest.
Arguments:
- tokens: bfloat16 [8192, 2048], P('expert', 'tensor'), may hold values from -6 to 6
- grad_out: bfloat16 [8192, 2048], P('expert', 'tensor'), may hold values from -6 to 6
- route_weights: float32 [8192, 8], P('expert'), may hold values from 0.02 to 0.5
- expert_ids: int32 [8192, 8], P('expert'), may hold values from 0 to 127, all different within a row; in each aligned block of 128 rows (0 to 127, 128 to 255, ...) at most 12 rows name the same one
- gate_weight: bfloat16 [128, 2048, 768], P('expert', None, 'tensor'), may hold values from -0.125 to 0.125
- up_weight: bfloat16 [128, 2048, 768], P('expert', None, 'tensor'), may hold values from -0.125 to 0.125
- down_weight: bfloat16 [128, 768, 2048], P('expert', 'tensor'), may hold values from -0.21875 to 0.21875
- gate_adapter_first: bfloat16 [128, 2048, 64], P('expert'), may hold values from -0.125 to 0.125
- gate_adapter_second: bfloat16 [128, 64, 768], P('expert', None, 'tensor'), may hold values from -0.75 to 0.75
- up_adapter_first: bfloat16 [128, 2048, 64], P('expert'), may hold values from -0.125 to 0.125
- up_adapter_second: bfloat16 [128, 64, 768], P('expert', None, 'tensor'), may hold values from -0.75 to 0.75
- down_adapter_first: bfloat16 [128, 768, 64], P('expert', 'tensor'), may hold values from -0.21875 to 0.21875
- down_adapter_second: bfloat16 [128, 64, 2048], P('expert'), may hold values from -0.75 to 0.75
Outputs:
- grad_tokens: bfloat16 [8192, 2048], P('expert', 'tensor')
- gate_first_gradient: float32 [128, 2048, 64], P('expert', 'tensor')
- gate_second_gradient: float32 [128, 64, 768], P('expert', None, 'tensor')
- up_first_gradient: float32 [128, 2048, 64], P('expert', 'tensor')
- up_second_gradient: float32 [128, 64, 768], P('expert', None, 'tensor')
- down_first_gradient: float32 [128, 768, 64], P('expert', 'tensor')
- down_second_gradient: float32 [128, 64, 2048], P('expert', None, 'tensor')
Inputs may be any that keep to these rules, and one draw needn't show every extreme that they name: `expert_ids`: each token names 8 different experts. Among the 128 rows of one device no expert is named more than 12 times, a bound that some block reaches.
All inputs are finite; a program needn't handle non-finite values.
Results may differ from a plain program's by a relative error of at most 0.012.
Values may be sent and summed in bfloat16 or wider, within the bound.
A program may use at most 128 MiB of HBM per device.

v0:
```python
import jax
import jax.numpy as jnp
from jax import lax
from jax.sharding import PartitionSpec as P

adapter_scale = 0.5


def side_by_side(arrays, axis, split_dim, concat_dim, along):
    widths = [a.shape[along] for a in arrays]
    both = jnp.concatenate(arrays, axis=along)
    result = lax.all_to_all(both, axis, split_axis=split_dim, concat_axis=concat_dim, tiled=True)
    return tuple(jnp.split(result, [sum(widths[:k]) for k in range(1, len(widths))], axis=along))


def sent_together(arrays, axis, dim, along):
    widths = [a.shape[along] for a in arrays]
    both = jnp.concatenate(arrays, axis=along)
    result = lax.all_gather(both, axis, axis=dim, tiled=True)
    return tuple(jnp.split(result, [sum(widths[:k]) for k in range(1, len(widths))], axis=along))


def from_everyone(shard, axis):
    peers = lax.axis_size(axis)
    return lax.all_to_all(
        jnp.broadcast_to(shard[None], (peers, *shard.shape)), axis, 0, 0, tiled=True
    )


def over_copies(shard, axis):
    return from_everyone(shard, axis).astype(jnp.float32).sum(axis=0)


def slot_positions(expert_ids, experts_all, capacity):
    tok_rows = expert_ids.shape[0]
    numbers = lax.broadcasted_iota(jnp.int32, (1, 1, experts_all), 2)
    picked = jnp.sum((expert_ids[:, :, None] == numbers).astype(jnp.float32), axis=1).astype(
        jnp.bfloat16
    )
    row_index = lax.broadcasted_iota(jnp.int32, (tok_rows, tok_rows), 0)
    col_index = lax.broadcasted_iota(jnp.int32, (tok_rows, tok_rows), 1)
    earlier = (row_index > col_index).astype(jnp.bfloat16)
    before = jnp.dot(earlier, picked, preferred_element_type=jnp.float32)
    slot_index = jnp.take_along_axis(before, expert_ids, axis=1).astype(jnp.int32)
    return expert_ids * capacity + slot_index


def fill_slots(values, positions, slot_count):
    width = values.shape[-1]
    flat = values.reshape(-1, width)
    return jnp.zeros((slot_count, width), values.dtype).at[positions.reshape(-1)].set(flat)


def local(
    tokens,
    grad_out,
    route_weights,
    expert_ids,
    gate_weight,
    up_weight,
    down_weight,
    gate_adapter_first,
    gate_adapter_second,
    up_adapter_first,
    up_adapter_second,
    down_adapter_first,
    down_adapter_second,
):
    single_float = jnp.float32
    brain_float_half = jnp.bfloat16
    tok_rows, top_count = expert_ids.shape
    local_experts = gate_weight.shape[0]
    sources = lax.axis_size("expert")
    experts_all = local_experts * sources
    capacity = 3 * tok_rows * top_count // (2 * experts_all)
    slot_count = experts_all * capacity
    positions = slot_positions(expert_ids, experts_all, capacity)
    width = tokens.shape[1]
    spread_in = jnp.broadcast_to(tokens[:, None, :], (tok_rows, top_count, width))
    scaled = (route_weights[:, :, None] * grad_out[:, None, :].astype(single_float)).astype(
        brain_float_half
    )
    send_in = fill_slots(spread_in, positions, slot_count)
    send_grad = fill_slots(scaled, positions, slot_count)
    part_in, part_grad = side_by_side((send_in, send_grad), "expert", 0, 0, 1)
    recv_in, recv_grad = sent_together((part_in, part_grad), "tensor", 1, 0)
    hidden_width = recv_in.shape[1]
    routed_input = recv_in.reshape(sources, local_experts, capacity, hidden_width)
    routed_gradient = recv_grad.reshape(sources, local_experts, capacity, hidden_width)
    slice_width = hidden_width // lax.axis_size("tensor")
    slice_start = lax.axis_index("tensor") * slice_width
    adapter_gate_term = jnp.einsum(
        "mbtk,bkz->mbtz", routed_input, gate_adapter_first, preferred_element_type=single_float
    ).astype(brain_float_half)
    adapter_up_term = jnp.einsum(
        "mbtk,bkz->mbtz", routed_input, up_adapter_first, preferred_element_type=single_float
    ).astype(brain_float_half)
    gate_activation = jnp.einsum(
        "secd,edf->secf", routed_input, gate_weight, preferred_element_type=single_float
    )
    gate_activation = gate_activation + adapter_scale * jnp.einsum(
        "imal,mlt->imat",
        adapter_gate_term,
        gate_adapter_second,
        preferred_element_type=single_float,
    )
    up_activation = jnp.einsum(
        "secd,edf->secf", routed_input, up_weight, preferred_element_type=single_float
    )
    up_activation = up_activation + adapter_scale * jnp.einsum(
        "imal,mlt->imat", adapter_up_term, up_adapter_second, preferred_element_type=single_float
    )
    sigma = jax.nn.sigmoid(gate_activation)
    active = gate_activation * sigma
    hidden_activation = (active * up_activation).astype(brain_float_half)
    down_part = jnp.einsum(
        "secf,efr->secr", hidden_activation, down_adapter_first, preferred_element_type=single_float
    )
    down_total = over_copies(down_part.astype(jnp.bfloat16), "tensor").astype(jnp.float32)
    backward_adapter_term = jnp.einsum(
        "secd,erd->secr", routed_gradient, down_adapter_second, preferred_element_type=single_float
    ).astype(brain_float_half)
    hidden_gradient = jnp.einsum(
        "secd,efd->secf", routed_gradient, down_weight, preferred_element_type=single_float
    )
    hidden_gradient = hidden_gradient + adapter_scale * jnp.einsum(
        "oamh,ath->oamt",
        backward_adapter_term,
        down_adapter_first,
        preferred_element_type=single_float,
    )
    gate_gradient = (
        hidden_gradient * up_activation * sigma * (1.0 + gate_activation * (1.0 - sigma))
    ).astype(brain_float_half)
    upward_gradient = (hidden_gradient * active).astype(brain_float_half)
    gate_part = jnp.einsum(
        "secf,erf->secr", gate_gradient, gate_adapter_second, preferred_element_type=single_float
    )
    up_part = jnp.einsum(
        "secf,erf->secr", upward_gradient, up_adapter_second, preferred_element_type=single_float
    )
    joined_weight = jnp.concatenate(
        (gate_weight, up_weight, gate_adapter_first, up_adapter_first), axis=2
    )
    joined_grad = jnp.concatenate(
        (
            gate_gradient,
            upward_gradient,
            gate_part.astype(brain_float_half) * adapter_scale,
            up_part.astype(brain_float_half) * adapter_scale,
        ),
        axis=3,
    )
    input_portion = (
        jnp.einsum(
            "secf,edf->secd", joined_grad, joined_weight, preferred_element_type=single_float
        )
        .astype(brain_float_half)
        .reshape(slot_count, hidden_width)
    )
    gate_total, up_total = (
        over_copies(gate_part.astype(jnp.bfloat16), "tensor").astype(jnp.float32),
        over_copies(up_part.astype(jnp.bfloat16), "tensor").astype(jnp.float32),
    )
    in_slice = lax.dynamic_slice_in_dim(routed_input, slice_start, slice_width, 3)
    grad_slice = lax.dynamic_slice_in_dim(routed_gradient, slice_start, slice_width, 3)
    gate_first_gradient = adapter_scale * jnp.einsum(
        "secd,secr->edr",
        in_slice,
        gate_total.astype(brain_float_half),
        preferred_element_type=single_float,
    )
    up_first_gradient = adapter_scale * jnp.einsum(
        "secd,secr->edr",
        in_slice,
        up_total.astype(brain_float_half),
        preferred_element_type=single_float,
    )
    gate_second_gradient = adapter_scale * jnp.einsum(
        "zdbq,zdbx->dqx", adapter_gate_term, gate_gradient, preferred_element_type=single_float
    )
    up_second_gradient = adapter_scale * jnp.einsum(
        "zdbq,zdbx->dqx", adapter_up_term, upward_gradient, preferred_element_type=single_float
    )
    down_first_gradient = adapter_scale * jnp.einsum(
        "qoax,qoap->oxp",
        hidden_activation,
        backward_adapter_term,
        preferred_element_type=single_float,
    )
    down_second_gradient = adapter_scale * jnp.einsum(
        "secr,secd->erd",
        down_total.astype(brain_float_half),
        grad_slice,
        preferred_element_type=single_float,
    )
    reduced = lax.psum_scatter(
        input_portion.astype(single_float).astype(jnp.bfloat16),
        "tensor",
        scatter_dimension=1,
        tiled=True,
    ).astype(jnp.float32)
    returned = lax.all_to_all(
        reduced.astype(jnp.bfloat16), "expert", split_axis=0, concat_axis=0, tiled=True
    ).astype(reduced.dtype)
    grad_tokens = jnp.sum(returned[positions], axis=1).astype(brain_float_half)
    return (
        grad_tokens,
        gate_first_gradient,
        gate_second_gradient,
        up_first_gradient,
        up_second_gradient,
        down_first_gradient,
        down_second_gradient,
    )


def solution(mesh):
    return jax.shard_map(
        local,
        mesh=mesh,
        in_specs=(
            P("expert", "tensor"),
            P("expert", "tensor"),
            P("expert", None),
            P("expert", None),
            P("expert", None, "tensor"),
            P("expert", None, "tensor"),
            P("expert", "tensor", None),
            P("expert", None, None),
            P("expert", None, "tensor"),
            P("expert", None, None),
            P("expert", None, "tensor"),
            P("expert", "tensor", None),
            P("expert", None, None),
        ),
        out_specs=(
            P("expert", "tensor"),
            P("expert", "tensor", None),
            P("expert", None, "tensor"),
            P("expert", "tensor", None),
            P("expert", None, "tensor"),
            P("expert", "tensor", None),
            P("expert", None, "tensor"),
        ),
        check_vma=False,
    )
```

profile of v0, /device:TPU:24, one launch (start us, length us, event | category | flops | bytes accessed | tf_op | source)
XLA Modules:
  0.0 454.0 jit_solution(12641412840922237685)
XLA Ops:
  10.3 6.8 %gather_fusion.1 = f32[1024]{0:T(1024)S(1)} fusion(f32[128,128]{1,0:T(8,128)S(1)} %fusion.80, s32[1024]{0:T(1024)S(1)} %reshape.100), kind=kCustom, calls=%fused_computation.1 | custom fusion | bytes 16384 | tf_op jit(solution)/shard_map/jit(take_along_axis)/gather | solution.py:44
  17.5 5.6 %scatter_custom_fusion = bf16[1536,512]{1,0:T(8,128)(2,1)S(1)} fusion(s32[1024]{0:T(1024)S(1)} %bitcast.204, bf16[]{:T(256)} %constant.14.clone.1, bf16[128,512]{1,0:T(8,128)(2,1)S(1)} %copy-done.21), kind=kCustom, calls=%fused_computation.80 | custom fusion | bytes 1703938 | tf_op jit(solution)/shard_map/scatter | solution.py:51
  23.1 6.8 %scatter_custom_fusion.1 = bf16[1536,512]{1,0:T(8,128)(2,1)} fusion(s32[1024]{0:T(1024)S(1)} %bitcast.205, f32[128,512]{1,0:T(8,128)S(1)} %convert_element_type.93, f32[1024]{0:T(1024)S(1)} %mul.92, bf16[]{:T(256)} %constant.14.clone.1), kind=kCustom, calls=%fused_computation.79 | custom fusion | flops 1048576 | bytes 1839106 | tf_op jit(solution)/shard_map/scatter | solution.py:51
  31.7 86.5 %all_to_all.36 = bf16[64,24,1024]{2,1,0:T(8,128)(2,1)S(1)} all-to-all(bf16[64,24,1024]{2,1,0:T(8,128)(2,1)S(1)} %bitcast.202), channel_id=1, replica_groups=mesh['expert'=64,'tensor'=4] {'expert'}, dimensions={0} | all-to-all | bytes 6291456 | tf_op jit(solution)/shard_map/all_to_all | solution.py:12
  131.7 73.7 %all-gather.2.cloned.1.call-done = bf16[3072,2048]{1,0:T(8,128)(2,1)} async-done(((bf16[3072,512]{1,0:T(8,128)(2,1)}), bf16[3072,2048]{1,0:T(8,128)(2,1)}) %all-gather.2.cloned.1.call-update) | async-done | bytes 12582928 | tf_op jit(solution)/shard_map/all_gather | solution.py:19
  205.4 10.7 %fusion.86 = (bf16[1536,2048]{1,0:T(8,128)(2,1)}, bf16[1536,2048]{1,0:T(8,128)(2,1)}) fusion(bf16[3072,2048]{1,0:T(8,128)(2,1)} %all-gather.2.cloned.1.call-done), kind=kLoop, calls=%fused_computation.113 | loop fusion | bytes 25165824 | tf_op jit(solution)/shard_map/split | solution.py:20
  216.1 10.6 %reshape.89 = bf16[64,2,12,2048]{3,2,1,0:T(8,128)(2,1)} reshape(bf16[1536,2048]{1,0:T(8,128)(2,1)} %get-tuple-element.9) | data formatting | bytes 12582912 | tf_op jit(solution)/shard_map/reshape | solution.py:88
  226.8 6.9 %copy.151 = bf16[64,2,12,2048]{3,0,2,1:T(8,128)(2,1)S(1)} copy(bf16[64,2,12,2048]{3,2,1,0:T(8,128)(2,1)} %reshape.89) | data formatting | bytes 12582912 | tf_op jit(solution)/shard_map/reshape | solution.py:88
  244.0 11.1 %reshape.88 = bf16[64,2,12,2048]{3,2,1,0:T(8,128)(2,1)} reshape(bf16[1536,2048]{1,0:T(8,128)(2,1)} %get-tuple-element.10) | data formatting | bytes 12582912 | tf_op jit(solution)/shard_map/reshape | solution.py:89
  255.1 6.9 %copy.149 = bf16[64,2,12,2048]{3,0,2,1:T(8,128)(2,1)S(1)} copy(bf16[64,2,12,2048]{3,2,1,0:T(8,128)(2,1)} %reshape.88) | data formatting | bytes 12582912 | tf_op jit(solution)/shard_map/reshape | solution.py:89
  272.2 8.5 %convert_bitcast_fusion = bf16[64,2,12,2048]{3,0,2,1:T(8,128)(2,1)} fusion(bf16[2,2048,64]{2,1,0:T(8,128)(2,1)} %copy.143, bf16[2,2048,64]{2,1,0:T(8,128)(2,1)S(1)} %copy-done.13, bf16[2,2048,192]{2,1,0:T(8,128)(2,1)} %copy.141, bf16[2,2048,192]{2,1,0:T(8,128)(2,1)S(1)} %copy-done.7, bf16[64,2,12,64]{3,0,2,1:T(8,128)(2,1)S(1)} %get-tuple-element.16, ...), kind=kOutput, calls=%fused_computation.4 | convolution fusion | flops 3247439872 | bytes 12058624 | tf_op jit(solution)/shard_map/secf,edf->secd/dot_general | solution.py:155
  280.6 9.7 %copy.155 = bf16[64,2,12,2048]{3,2,1,0:T(8,128)(2,1)} copy(bf16[64,2,12,2048]{3,0,2,1:T(8,128)(2,1)} %convert_bitcast_fusion) | data formatting | bytes 12582912 | tf_op jit(solution)/shard_map/convert_element_type | solution.py:158
  290.3 10.7 %reshape.90 = bf16[1536,2048]{1,0:T(8,128)(2,1)} reshape(bf16[64,2,12,2048]{3,2,1,0:T(8,128)(2,1)} %copy.155) | data formatting | bytes 12582912 | tf_op jit(solution)/shard_map/reshape | solution.py:159
  305.0 4.2 all-to-all-start.4
  313.1 9.4 %all-to-all-done.4 = bf16[4,2,49152]{2,1,0:T(2,128)(2,1)} async-done(((bf16[4,2,49152]{2,1,0:T(2,128)(2,1)}), bf16[4,2,49152]{2,1,0:T(2,128)(2,1)}, u32[]{:S(2)}, u32[]{:S(2)}) %all-to-all-start.4) | async-done | bytes 786464 | tf_op jit(solution)/shard_map/all_to_all | solution.py:25
  322.4 4.2 all-to-all-start.3
  330.4 14.5 %all-to-all-done.3 = bf16[4,2,49152]{2,1,0:T(2,128)(2,1)} async-done(((bf16[4,2,49152]{2,1,0:T(2,128)(2,1)}), bf16[4,2,49152]{2,1,0:T(2,128)(2,1)}, u32[]{:S(2)}, u32[]{:S(2)}) %all-to-all-start.3) | async-done | bytes 786464 | tf_op jit(solution)/shard_map/all_to_all | solution.py:25
  344.9 26.2 %all_to_all.37 = bf16[4,2,49152]{2,1,0:T(2,128)(2,1)} all-to-all(bf16[4,2,49152]{2,1,0:T(2,128)(2,1)} %reshape.149), channel_id=1, replica_groups=mesh['expert'=64,'tensor'=4] {'tensor'}, dimensions={0} | all-to-all | bytes 1572864 | tf_op jit(solution)/shard_map/all_to_all | solution.py:25
  371.2 12.5 %reduce-scatter.2.cloned.1.call-done = bf16[1536,512]{1,0:T(8,128)(2,1)} async-done(((bf16[1536,2048]{1,0:T(8,128)(2,1)}), bf16[1536,512]{1,0:T(8,128)(2,1)}) %reduce-scatter.2.cloned.1.call-update) | async-done | bytes 1572880 | tf_op jit(solution)/shard_map/reduce_scatter | solution.py:197
  383.7 10.8 %all-to-all-start.1 = ((bf16[64,24,512]{2,1,0:T(8,128)(2,1)}), bf16[64,24,512]{2,1,0:T(8,128)(2,1)S(1)}, u32[]{:S(2)}, u32[]{:S(2)}) async-start(bf16[64,24,512]{2,1,0:T(8,128)(2,1)} %bitcast.203), calls=%async_computation.2 | async-start | bytes 3145728 | tf_op jit(solution)/shard_map/all_to_all | solution.py:203
  403.1 4.0 reshape.152
  407.0 4.0 reshape.150
  420.9 13.7 %all-to-all-done.1 = bf16[64,24,512]{2,1,0:T(8,128)(2,1)S(1)} async-done(((bf16[64,24,512]{2,1,0:T(8,128)(2,1)}), bf16[64,24,512]{2,1,0:T(8,128)(2,1)S(1)}, u32[]{:S(2)}, u32[]{:S(2)}) %all-to-all-start.1) | async-done | bytes 1572896 | tf_op jit(solution)/shard_map/all_to_all | solution.py:203
  436.8 7.3 %gather_fusion = f32[1024,512]{1,0:T(8,128)} fusion(f32[1536,512]{1,0:T(8,128)} %bitcast_convert_fusion, s32[1024]{0:T(1024)S(1)} %broadcast_clamp_fusion), kind=kCustom, calls=%fused_computation | custom fusion | bytes 4198400 | tf_op jit(solution)/shard_map/gather | solution.py:206
  (111 shorter events, 74.1 us)
Async XLA Ops:
  7.2 257.4 %copy-start = (bf16[2,192,2048]{2,1,0:T(8,128)(2,1)S(1)}, bf16[2,192,2048]{2,1,0:T(8,128)(2,1)}, u32[]{:S(2)}) copy-start(bf16[2,192,2048]{2,1,0:T(8,128)(2,1)} %param.19) | copy-start | bytes 4718596
  7.2 198.3 %all-gather.2.cloned.1.call-start = ((), (), s32[]{:S(2)}) async-start(), calls=%async_computation.6 | async-start | bytes 15728640 | tf_op jit(solution)/shard_map/all_gather | solution.py:19
  10.3 7.0 %copy-start.23 = (s32[128,8]{0,1:T(8,128)S(1)}, s32[128,8]{0,1:T(8,128)}, u32[]{:S(2)}) copy-start(s32[128,8]{0,1:T(8,128)} %param.16) | copy-start | bytes 12292
  10.3 7.2 %copy-start.20 = (bf16[128,512]{1,0:T(8,128)(2,1)S(1)}, bf16[128,512]{1,0:T(8,128)(2,1)}, u32[]{:S(2)}) copy-start(bf16[128,512]{1,0:T(8,128)(2,1)} %param.14) | copy-start | bytes 393220
  10.3 7.2 %copy-start.21 = (bf16[128,512]{1,0:T(8,128)(2,1)S(1)}, bf16[128,512]{1,0:T(8,128)(2,1)}, u32[]{:S(2)}) copy-start(bf16[128,512]{1,0:T(8,128)(2,1)} %param.13) | copy-start | bytes 393220
  120.3 4.9 %copy-start.8 = (bf16[2,2048,192]{1,2,0:T(8,128)(2,1)S(1)}, bf16[2,2048,192]{1,2,0:T(8,128)(2,1)}, u32[]{:S(2)}) copy-start(bf16[2,2048,192]{1,2,0:T(8,128)(2,1)} %param.17) | copy-start | bytes 4718596
  120.3 263.4 %reduce-scatter.2.cloned.1.call-start = ((), (), s32[]{:S(2)}) async-start(), calls=%async_computation.7 | async-start | bytes 7864320 | tf_op jit(solution)/shard_map/reduce_scatter | solution.py:197
  226.8 6.9 %copy-start.14 = (bf16[2,2048,64]{1,2,0:T(8,128)(2,1)S(1)}, bf16[2,2048,64]{1,2,0:T(8,128)(2,1)}, u32[]{:S(2)}) copy-start(bf16[2,2048,64]{1,2,0:T(8,128)(2,1)} %param.20) | copy-start | bytes 1572868
  233.7 7.3 %copy-start.2 = (bf16[64,2,12,2048]{3,0,2,1:T(8,128)(2,1)}, bf16[64,2,12,2048]{3,0,2,1:T(8,128)(2,1)S(1)}, u32[]{:S(2)}) copy-start(bf16[64,2,12,2048]{3,0,2,1:T(8,128)(2,1)S(1)} %copy.151) | copy-start | bytes 18874372
  238.0 3.0 copy-start.9
  255.1 6.9 %copy-start.24 = (bf16[2,64,2048]{2,1,0:T(8,128)(2,1)S(1)}, bf16[2,64,2048]{2,1,0:T(8,128)(2,1)}, u32[]{:S(2)}) copy-start(bf16[2,64,2048]{2,1,0:T(8,128)(2,1)} %param.25) | copy-start | bytes 1572868
  262.0 2.6 copy-start.3
  264.6 2.2 copy-start.11
  264.6 1.8 copy-start.10
  264.6 1.8 copy-start.17
  269.9 2.3 copy-start.6
  269.9 2.3 copy-start.7
  269.9 2.3 copy-start.13
  305.0 17.4 %all-to-all-start.4 = ((bf16[4,2,49152]{2,1,0:T(2,128)(2,1)}), bf16[4,2,49152]{2,1,0:T(2,128)(2,1)}, u32[]{:S(2)}, u32[]{:S(2)}) async-start(bf16[4,2,49152]{2,1,0:T(2,128)(2,1)} %reshape.153), calls=%async_computation.5 | async-start | bytes 1572864 | tf_op jit(solution)/shard_map/all_to_all | solution.py:25
  322.4 22.5 %all-to-all-start.3 = ((bf16[4,2,49152]{2,1,0:T(2,128)(2,1)}), bf16[4,2,49152]{2,1,0:T(2,128)(2,1)}, u32[]{:S(2)}, u32[]{:S(2)}) async-start(bf16[4,2,49152]{2,1,0:T(2,128)(2,1)} %reshape.151), calls=%async_computation.4 | async-start | bytes 1572864 | tf_op jit(solution)/shard_map/all_to_all | solution.py:25
  383.7 51.0 %all-to-all-start.1 = ((bf16[64,24,512]{2,1,0:T(8,128)(2,1)}), bf16[64,24,512]{2,1,0:T(8,128)(2,1)S(1)}, u32[]{:S(2)}, u32[]{:S(2)}) async-start(bf16[64,24,512]{2,1,0:T(8,128)(2,1)} %bitcast.203), calls=%async_computation.2 | async-start | bytes 3145728 | tf_op jit(solution)/shard_map/all_to_all | solution.py:203
  396.2 3.2 copy-start.12
  411.0 1.9 copy-start.5
  436.8 10.1 %copy-start.1 = (bf16[2,192,2048]{2,1,0:T(8,128)(2,1)S(1)}, bf16[2,192,2048]{2,1,0:T(8,128)(2,1)}, u32[]{:S(2)}) copy-start(bf16[2,192,2048]{2,1,0:T(8,128)(2,1)} %param.19) | copy-start | bytes 4718596
  (7 other events, 8.5 us)
Sparse Core Ops, SparseCore 0:
  120.4 85.0 all-gather.1
  301.2 82.4 reduce-scatter.1
where the time goes:
time: 463 us; the launch traced here: 454 us
  local copies, waits for them, and re-layouts  127 us (27%)
  waiting for transfers between devices  124 us (27%)
  blocking collectives  113 us (24%)
  matrix products  38.6 us (8%)
  starting transfers between devices  19.3 us (4%)
  other arithmetic  17.5 us (4%)
  between operations  14.7 us (3%)
    all_to_all x1, blocking collectives, side_by_side(): lax.all_to_all(both, axis, split_axis=split_dim, concat_axis=concat_dim,...  86.5 us
    all_gather x1, waiting for transfers between devices, sent_together(): result = lax.all_gather(both, axis, axis=dim, tiled=True)  73.7 us
    unnamed x67, local copies, waits for them, and re-layouts  38.7 us
    all_to_all x1, blocking collectives, from_everyone(): lax.all_to_all(jnp.broadcast_to(shard[None], (peers, *shard.shape)), axis...  26.2 us
    all_to_all x2, waiting for transfers between devices, from_everyone(): lax.all_to_all(jnp.broadcast_to(shard[None], (peers, *shard.shape)), axis...  23.9 us
    reshape x2, local copies, waits for them, and re-layouts, local(): recv_grad.reshape(sources, local_experts, capacity, hidden_width)  18 us
    reshape x2, local copies, waits for them, and re-layouts, local(): recv_in.reshape(sources, local_experts, capacity, hidden_width)  17.5 us
    all_to_all x1, waiting for transfers between devices, local(): lax.all_to_all(reduced.astype(jnp.bfloat16), 'expert', split_axis=0, conc...  13.7 us
  transfers between devices with their start and end apart: 5, of which 5 were waited for; matrix products, arithmetic and copies ran while one was open for 10% of the time, Pallas kernels for 0%

commit v1 on v0

v1 whole, which is shorter than its diff:
```python
import functools

import jax
import jax.numpy as jnp
import numpy as np
from jax import lax
from jax.experimental import pallas as pl
from jax.experimental.pallas import tpu as pltpu
from jax.sharding import PartitionSpec as P

MESH = pl.DeviceIdType.MESH
F32 = jnp.float32
BF16 = jnp.bfloat16
PAIRS = ((0, 1), (-1, 2), (-2, 3), (-3, 4))
CAP = 12
FAR = 4096.0
VMEM_LIMIT = 58 * 2**20


def place():
    expert = lax.axis_index("expert")
    tensor = lax.axis_index("tensor")
    y = expert % 4
    z = (expert // 4) % 8
    xl = expert // 32
    xh = tensor // 2
    core = tensor % 2
    return xl, xh, y, z, core


def device(xl, xh, y, z, core):
    return (xl * 32 + z * 4 + y, xh * 2 + core)


def rem_copy(src, dst, send, recv, target):
    return pltpu.make_async_remote_copy(
        src_ref=src, dst_ref=dst, send_sem=send, recv_sem=recv,
        device_id=target, device_id_type=MESH,
    )


def side(xl, xh, step):
    x = (xh * 2 + xl + step) % 4
    return x % 2, x // 2


def greet(targets):
    barrier = pltpu.get_barrier_semaphore()
    for target in targets:
        pl.semaphore_signal(barrier, inc=1, device_id=target, device_id_type=MESH)
    pl.semaphore_wait(barrier, len(targets))


def one_hot(table, base, info_a, info_b, pos_only):
    ids = table + base
    hot = jnp.zeros((48, 256), F32)
    weight = jnp.zeros((48, 256), F32)
    for k in range(8):
        pos = jnp.concatenate([info_a[k : k + 1], info_b[k : k + 1] + FAR], axis=1)
        match = ids == pos
        hot = jnp.where(match, 1.0, hot)
        if not pos_only:
            w = jnp.concatenate([info_a[8 + k : 9 + k], info_b[8 + k : 9 + k]], axis=1)
            weight = jnp.where(match, w, weight)
    if pos_only:
        return hot
    return hot, jnp.sum(weight, axis=1, keepdims=True)


def dispatch_kernel(
    tok_ref, grad_ref, ids_ref, rw_ref, table_ref,
    f_ref, info_ref,
    zb, stage_same, stage_diff, relay,
    info_send, info_recv, swap_sem, ring_send, ring_recv,
    same_send, same_recv, diff_send, diff_recv, x_send, x_recv, core_send, core_recv,
):
    xl, xh, y, z, core = place()
    here = functools.partial(device, xl, xh)
    z_others = [here(y, (z + d) % 8, core) for d in range(1, 8)]
    y_others = [here((y + j) % 4, z, core) for j in range(1, 4)]
    x_sides = [device(*side(xl, xh, s), y, z, core) for s in (1, 3)]
    x_far = device(xl, 1 - xh, y, z, core)
    partner = here(y, z, 1 - core)

    zb[0, 0, :, 0:512] = tok_ref[...]
    zb[0, 0, :, 512:1024] = grad_ref[...]

    ids = ids_ref[...]
    numbers = lax.broadcasted_iota(jnp.int32, (128, 128), 0)
    picked = jnp.zeros((128, 128), F32)
    for k in range(8):
        picked = jnp.where(ids[k : k + 1] == numbers, 1.0, picked)
    later = lax.broadcasted_iota(jnp.int32, (128, 128), 1) > numbers
    before = jnp.dot(
        picked.astype(BF16), jnp.where(later, 1.0, 0.0).astype(BF16), preferred_element_type=F32
    )
    for k in range(8):
        slot = jnp.sum(jnp.where(ids[k : k + 1] == numbers, before, 0.0), axis=0, keepdims=True)
        info_ref[0, k : k + 1, :] = ids[k : k + 1].astype(F32) * CAP + slot
    info_ref[0, 8:16, :] = rw_ref[...]

    greet(z_others + y_others + x_sides + [x_far, partner])

    swap = rem_copy(zb.at[0, 0], zb.at[0, 1], swap_sem.at[0], swap_sem.at[1], x_far)
    swap.start()
    down, up = here(y, (z + 7) % 8, core), here(y, (z + 1) % 8, core)

    def ring(direction, h, chunk):
        if direction == 0:
            src, dst = (h - 1) % 8, h % 8
        else:
            src, dst = (1 - h) % 8, (-h) % 8
        n = (h - 1) * 2 + chunk
        return rem_copy(
            zb.at[src, chunk], zb.at[dst, chunk],
            ring_send.at[direction, n], ring_recv.at[direction, n],
            down if direction == 0 else up,
        )

    ring(0, 1, 0).start()
    ring(1, 1, 0).start()
    infos = []
    for d in range(1, 8):
        copy = rem_copy(
            info_ref.at[0], info_ref.at[(8 - d) % 8], info_send.at[d - 1], info_recv.at[d - 1],
            z_others[d - 1],
        )
        copy.start()
        infos.append(copy)
    swap.wait_recv()
    ring(0, 1, 1).start()
    ring(1, 1, 1).start()
    for copy in infos:
        copy.wait_recv()

    def advance(direction, h, chunk):
        ring(direction, h, chunk).wait_recv()
        nxt = h + 1
        if nxt < 4 or (nxt == 4 and chunk == direction):
            ring(direction, nxt, chunk).start()

    def same_copy(p, j):
        ys = (y + j) % 4
        return rem_copy(
            stage_same.at[p, j - 1], f_ref.at[core, :, :, p, xl, y],
            same_send.at[p, j - 1], same_recv.at[p, j - 1], here(ys, z, core),
        )

    def diff_copy(p, j):
        ys = (y + j) % 4
        return rem_copy(
            stage_diff.at[p, j - 1], relay.at[p, :, y],
            diff_send.at[p, j - 1], diff_recv.at[p, j - 1], here(ys, z, core),
        )

    def x_copy(p, s):
        return rem_copy(
            relay.at[p], f_ref.at[core, xh, :, p, xl],
            x_send.at[p, s], x_recv.at[p, s], x_sides[s],
        )

    def core_copy(p, part):
        if part == 0:
            piece = f_ref.at[core, :, :, p, xl]
        else:
            from_xl, from_xh = side(xl, xh, (1, 3)[part - 1])
            piece = f_ref.at[core, from_xh, :, p, from_xl]
        return rem_copy(piece, piece, core_send.at[p, part], core_recv.at[p, part], partner)

    table = table_ref[...]

    def select(p):
        a, b = PAIRS[p][0] % 8, PAIRS[p][1] % 8
        info_a, info_b = info_ref[a], info_ref[b]
        own = jnp.concatenate([zb[a, 0], zb[b, 0]], axis=0)
        other = jnp.concatenate([zb[a, 1], zb[b, 1]], axis=0)

        def rows_of(hot, weight, x):
            rows = jnp.dot(hot.astype(BF16), x, preferred_element_type=F32)
            taken = rows[:, 0:512].astype(BF16)
            scaled = (rows[:, 512:1024] * weight).astype(BF16)
            return jnp.concatenate([taken, scaled], axis=1)

        for diff in (True, False):
            target_xl = 1 - xl if diff else xl
            hots, weights = [], []
            for j in range(4):
                base = ((target_xl * 64 + z * 8 + ((y + j) % 4) * 2) * CAP).astype(F32)
                hot, weight = one_hot(table, base, info_a, info_b, False)
                hots.append(hot)
                weights.append(weight)
            hot = jnp.concatenate(hots, axis=0)
            weight = jnp.concatenate(weights, axis=0)
            rows = rows_of(hot, weight, own).reshape(4, 2, 24, 1024)
            if diff:
                relay[p, :, y] = rows[0]
                for j in range(1, 4):
                    stage_diff[p, j - 1] = rows[j]
                    diff_copy(p, j).start()
            else:
                rows_b = rows_of(hot, weight, other).reshape(4, 2, 24, 1024)
                f_ref[core, xh, :, p, xl, y] = rows[0]
                f_ref[core, 1 - xh, :, p, xl, y] = rows_b[0]
                for j in range(1, 4):
                    stage_same[p, j - 1, xh] = rows[j]
                    stage_same[p, j - 1, 1 - xh] = rows_b[j]
                    same_copy(p, j).start()

    def forward(p):
        for j in range(1, 4):
            diff_copy(p, j).wait_recv()
        x_copy(p, 0).start()
        x_copy(p, 1).start()
        for j in range(1, 4):
            same_copy(p, j).wait_recv()
        core_copy(p, 0).start()

    def gather(p):
        for s in (0, 1):
            x_copy(p, 1 - s).wait_recv()
            core_copy(p, 1 + s).start()

    advance(0, 1, 0)
    advance(1, 1, 0)
    advance(0, 1, 1)
    advance(1, 1, 1)
    select(0)
    for h in (2, 3):
        advance(0, h, 0)
        advance(1, h, 0)
        advance(0, h, 1)
        advance(1, h, 1)
        select(h - 1)
        forward(h - 2)
        if h == 3:
            gather(0)
    ring(0, 4, 0).wait_recv()
    ring(1, 4, 1).wait_recv()
    select(3)
    forward(2)
    gather(1)
    forward(3)
    gather(2)
    gather(3)
    for p in range(4):
        for part in range(3):
            core_copy(p, part).wait_recv()

    swap.wait_send()
    for copy in infos:
        copy.wait_send()
    for direction in (0, 1):
        for h in range(1, 5):
            for chunk in (0, 1):
                if h < 4 or chunk == direction:
                    ring(direction, h, chunk).wait_send()
    for p in range(4):
        for j in range(1, 4):
            same_copy(p, j).wait_send()
            diff_copy(p, j).wait_send()
        for s in (0, 1):
            x_copy(p, s).wait_send()
        for part in range(3):
            core_copy(p, part).wait_send()


def dispatch(tokens, grad_out, ids, weights, table):
    vmem = pl.BlockSpec(memory_space=pltpu.VMEM)
    dma = pltpu.SemaphoreType.DMA
    return pl.pallas_call(
        dispatch_kernel,
        name="dispatch",
        out_shape=(
            jax.ShapeDtypeStruct((2, 2, 2, 4, 2, 4, 24, 1024), BF16),
            jax.ShapeDtypeStruct((8, 16, 128), F32),
        ),
        in_specs=[vmem] * 5,
        out_specs=(vmem, vmem),
        scratch_shapes=[
            pltpu.VMEM((8, 2, 128, 1024), BF16),
            pltpu.VMEM((4, 3, 2, 2, 24, 1024), BF16),
            pltpu.VMEM((4, 3, 2, 24, 1024), BF16),
            pltpu.VMEM((4, 2, 4, 24, 1024), BF16),
            dma((7,)), dma((7,)), dma((2,)), dma((2, 8)), dma((2, 8)),
            dma((4, 3)), dma((4, 3)), dma((4, 3)), dma((4, 3)),
            dma((4, 2)), dma((4, 2)), dma((4, 3)), dma((4, 3)),
        ],
        compiler_params=pltpu.CompilerParams(
            collective_id=0, has_side_effects=True, vmem_limit_bytes=VMEM_LIMIT
        ),
    )(tokens, grad_out, ids, weights, table)


def nt(a, b):
    return lax.dot_general(a, b, (((1,), (1,)), ((), ())), preferred_element_type=F32)


def tn(a, b):
    return lax.dot_general(a, b, (((0,), (0,)), ((), ())), preferred_element_type=F32)


def nn(a, b):
    return jnp.dot(a, b, preferred_element_type=F32)


PT = 2


def expert_kernel(
    f_ref, wg_ref, wu_ref, wd_ref, ag_ref, bg_ref, au_ref, bu_ref, ad_ref, bd_ref,
    p_ref, low_ref, gs_ref, us_ref, df_ref,
):
    rows = PT * 192

    def tile(n, carry):
        e, h = n // (4 // PT), n % (4 // PT)

        def take(cq, qh, lo):
            return f_ref[cq, qh, e, pl.ds(h * PT, PT), :, :, :, lo : lo + 512].reshape(rows, 512)

        x = jnp.concatenate([take(0, 0, 0), take(1, 0, 0), take(0, 1, 0), take(1, 1, 0)], axis=1)
        lg = nn(x, ag_ref[e]).astype(BF16)
        lu = nn(x, au_ref[e]).astype(BF16)
        gate = nn(x, wg_ref[e]) + 0.5 * nn(lg, bg_ref[e])
        up = nn(x, wu_ref[e]) + 0.5 * nn(lu, bu_ref[e])
        sigma = jax.nn.sigmoid(gate)
        active = gate * sigma
        hidden = (active * up).astype(BF16)
        down = nn(hidden, ad_ref[e]).astype(BF16)
        g = jnp.concatenate(
            [take(0, 0, 512), take(1, 0, 512), take(0, 1, 512), take(1, 1, 512)], axis=1
        )
        back = nt(g, bd_ref[e]).astype(BF16)
        gh = nt(g, wd_ref[e]) + 0.5 * nt(back, ad_ref[e])
        gg = (gh * up * sigma * (1.0 + gate * (1.0 - sigma))).astype(BF16)
        gu = (gh * active).astype(BF16)
        gp = nt(gg, bg_ref[e]).astype(BF16)
        upp = nt(gu, bu_ref[e]).astype(BF16)
        low_ref[e, pl.ds(h * rows, rows), 0:64] = down
        low_ref[e, pl.ds(h * rows, rows), 64:128] = gp
        low_ref[e, pl.ds(h * rows, rows), 128:192] = upp
        gs, us, df = 0.5 * tn(lg, gg), 0.5 * tn(lu, gu), 0.5 * tn(hidden, back)

        @pl.when(h == 0)
        def _():
            gs_ref[e] = gs
            us_ref[e] = us
            df_ref[e] = df

        @pl.when(h > 0)
        def _():
            gs_ref[e] += gs
            us_ref[e] += us
            df_ref[e] += df

        hgp, hup = gp * 0.5, upp * 0.5
        for q in range(4):
            cols = slice(q * 512, q * 512 + 512)
            part = nt(gg, wg_ref[e, cols]) + nt(gu, wu_ref[e, cols])
            part = part + (nt(hgp, ag_ref[e, cols]) + nt(hup, au_ref[e, cols]))
            p_ref[q % 2, q // 2, e, pl.ds(h * PT, PT)] = part.astype(BF16).reshape(PT, 2, 4, 24, 512)
        return carry

    lax.fori_loop(0, 2 * (4 // PT), tile, 0)


def experts(f, wg, wu, wd, ag, bg, au, bu, ad, bd):
    vmem = pl.BlockSpec(memory_space=pltpu.VMEM)
    return pl.pallas_call(
        expert_kernel,
        name="experts",
        out_shape=(
            jax.ShapeDtypeStruct((2, 2, 2, 4, 2, 4, 24, 512), BF16),
            jax.ShapeDtypeStruct((2, 768, 192), BF16),
            jax.ShapeDtypeStruct((2, 64, 192), F32),
            jax.ShapeDtypeStruct((2, 64, 192), F32),
            jax.ShapeDtypeStruct((2, 192, 64), F32),
        ),
        in_specs=[vmem] * 10,
        out_specs=(vmem,) * 5,
        compiler_params=pltpu.CompilerParams(vmem_limit_bytes=VMEM_LIMIT),
    )(f, wg, wu, wd, ag, bg, au, bu, ad, bd)


def return_kernel(
    p_ref, low_ref, f_ref, info_ref, table_ref,
    out_ref, gf_ref, uf_ref, ds_ref,
    r1, cps, cpx, xr, xs_stage, ys, yd, zs, zr, fin, rl, ls, rl2, tl,
    c_send, c_recv, s_send, s_recv, x_send, x_recv, d_send, d_recv, z_send, z_recv, l_send, l_recv, f_sem,
):
    xl, xh, y, z, core = place()
    here = functools.partial(device, xl, xh)
    y_others = [here((y + j) % 4, z, core) for j in range(1, 4)]
    x_sides = [device(*side(xl, xh, s), y, z, core) for s in (1, 3)]
    x_far = device(xl, 1 - xh, y, z, core)
    partner = here(y, z, 1 - core)
    down, up = here(y, (z + 7) % 8, core), here(y, (z + 1) % 8, core)
    greet([down, up] + y_others + x_sides + [x_far, partner])

    def core_copy(p):
        return rem_copy(
            p_ref.at[1 - core, :, :, p], r1.at[:, :, p], c_send.at[p], c_recv.at[p], partner
        )

    low_core = rem_copy(low_ref.at[1 - core], rl, l_send.at[0], l_recv.at[0], partner)
    low_far = rem_copy(ls, rl2, l_send.at[1], l_recv.at[1], x_far)
    low_back = rem_copy(tl.at[core], tl.at[core], l_send.at[2], l_recv.at[2], partner)
    core_copy(3).start()
    core_copy(2).start()
    low_core.start()
    core_copy(1).start()
    core_copy(0).start()

    def same_copy(p, j):
        return rem_copy(
            cps.at[p, j - 1], ys.at[p, y], s_send.at[p, j - 1], s_recv.at[p, j - 1],
            here((y + j) % 4, z, core),
        )

    def diff_copy(p, j):
        return rem_copy(
            xs_stage.at[p, j - 1], yd.at[p, y], d_send.at[p, j - 1], d_recv.at[p, j - 1],
            here((y + j) % 4, z, core),
        )

    def x_copy(p, s):
        _, to_xh = side(xl, xh, (1, 3)[s])
        return rem_copy(
            cpx.at[p, to_xh], xr.at[p, xh], x_send.at[p, s], x_recv.at[p, s], x_sides[s]
        )

    def chip_sum(p):
        core_copy(p).wait_recv()
        for qh in (0, 1):
            mine = p_ref[core, qh, :, p, 1 - xl].astype(F32)
            cpx[p, qh] = (mine + r1[qh, :, p, 1 - xl].astype(F32)).astype(BF16)
        x_copy(p, 0).start()
        x_copy(p, 1).start()
        for j in range(4):
            to = (y + j) % 4
            mine = p_ref[core, :, :, p, xl, to].astype(F32)
            total = (mine + r1[:, :, p, xl, to].astype(F32)).astype(BF16)
            if j == 0:
                ys[p, y] = total
            else:
                cps[p, j - 1] = total
                same_copy(p, j).start()

    def x_sum(p):
        x_copy(p, 0).wait_recv()
        x_copy(p, 1).wait_recv()
        for j in range(4):
            to = (y + j) % 4
            total = (xr[p, 0, :, to].astype(F32) + xr[p, 1, :, to].astype(F32)).astype(BF16)
            if j == 0:
                yd[p, y] = total
            else:
                xs_stage[p, j - 1] = total
                diff_copy(p, j).start()

    table = table_ref[...]

    def combine(p):
        a, b = PAIRS[p][0] % 8, PAIRS[p][1] % 8
        info_a, info_b = info_ref[a], info_ref[b]
        hot = []
        for target_xl in (xl, 1 - xl):
            hots = []
            for j in range(4):
                base = ((target_xl * 64 + z * 8 + j * 2) * CAP).astype(F32)
                hots.append(one_hot(table, base, info_a, info_b, True))
            hot.append(jnp.concatenate(hots, axis=0).astype(BF16))
        for j in range(1, 4):
            same_copy(p, j).wait_recv()
            diff_copy(p, j).wait_recv()
        own = tn(hot[0], ys[p, :, xh].reshape(192, 512)) + tn(hot[1], yd[p].reshape(192, 512))
        other = tn(hot[0], ys[p, :, 1 - xh].reshape(192, 512))
        return {PAIRS[p][0]: (own[0:128], other[0:128]), PAIRS[p][1]: (own[128:], other[128:])}

    def z_copy(direction, h):
        n = direction * 4 + h - 1
        to = up if direction == 0 else down
        if h == 1:
            src, dst = zs.at[n, direction], zr.at[n, direction]
        else:
            src, dst = zs.at[n], zr.at[n]
        return rem_copy(src, dst, z_send.at[n], z_recv.at[n], to)

    def z_hop(direction, h, parts):
        n = direction * 4 + h - 1
        for chunk in (0, 1):
            if h == 1 and chunk != direction:
                continue
            value = parts[chunk]
            if h > 2 or (h == 2 and chunk == direction):
                value = value + zr[n - 1, chunk].astype(F32)
            zs[n, chunk] = value.astype(BF16)
        z_copy(direction, h).start()

    chip_sum(3)
    chip_sum(2)
    low_core.wait_recv()
    ls[...] = (low_ref[core].astype(F32) + rl[...].astype(F32)).astype(BF16)
    low_far.start()
    x_sum(3)
    chip_sum(1)
    chip_sum(0)
    x_sum(2)
    far = combine(3)
    z_hop(0, 1, far[4])
    z_hop(1, 1, far[4])
    x_sum(1)
    low_far.wait_recv()
    tl[core] = (ls[...].astype(F32) + rl2[...].astype(F32)).astype(BF16)
    low_back.start()
    near = combine(2)
    z_copy(0, 1).wait_recv()
    z_hop(0, 2, near[3])
    z_copy(1, 1).wait_recv()
    z_hop(1, 2, far[-3])
    x_sum(0)
    far = near
    near = combine(1)
    z_copy(0, 2).wait_recv()
    z_hop(0, 3, near[2])
    z_copy(1, 2).wait_recv()
    z_hop(1, 3, far[-2])
    far = near
    near = combine(0)
    z_copy(0, 3).wait_recv()
    z_hop(0, 4, near[1])
    z_copy(1, 3).wait_recv()
    z_hop(1, 4, far[-1])

    low_back.wait_recv()
    for e in (0, 1):
        quarter = f_ref[core, xh, e].reshape(768, 1024)
        total = tl[e]
        both = 0.5 * tn(quarter[:, 0:512], total[:, 64:192])
        gf_ref[e] = both[:, 0:64]
        uf_ref[e] = both[:, 64:128]
        ds_ref[e] = 0.5 * tn(total[:, 0:64], quarter[:, 512:1024])

    z_copy(0, 4).wait_recv()
    z_copy(1, 4).wait_recv()
    home = [
        near[0][chunk] + zr[3, chunk].astype(F32) + zr[7, chunk].astype(F32) for chunk in (0, 1)
    ]
    fin[0] = home[1].astype(BF16)
    last = rem_copy(fin.at[0], fin.at[1], f_sem.at[0], f_sem.at[1], x_far)
    last.start()
    last.wait_recv()
    out_ref[...] = (home[0] + fin[1].astype(F32)).astype(BF16)

    last.wait_send()
    low_core.wait_send()
    low_far.wait_send()
    low_back.wait_send()
    for p in range(4):
        core_copy(p).wait_send()
        x_copy(p, 0).wait_send()
        x_copy(p, 1).wait_send()
        for j in range(1, 4):
            same_copy(p, j).wait_send()
            diff_copy(p, j).wait_send()
        z_copy(0, p + 1).wait_send()
        z_copy(1, p + 1).wait_send()


def send_back(p, low, f, info, table):
    vmem = pl.BlockSpec(memory_space=pltpu.VMEM)
    dma = pltpu.SemaphoreType.DMA
    return pl.pallas_call(
        return_kernel,
        name="send_back",
        out_shape=(
            jax.ShapeDtypeStruct((128, 512), BF16),
            jax.ShapeDtypeStruct((2, 512, 64), F32),
            jax.ShapeDtypeStruct((2, 512, 64), F32),
            jax.ShapeDtypeStruct((2, 64, 512), F32),
        ),
        in_specs=[vmem] * 5,
        out_specs=(vmem,) * 4,
        scratch_shapes=[
            pltpu.VMEM((2, 2, 4, 2, 4, 24, 512), BF16),
            pltpu.VMEM((4, 3, 2, 2, 24, 512), BF16),
            pltpu.VMEM((4, 2, 2, 4, 24, 512), BF16),
            pltpu.VMEM((4, 2, 2, 4, 24, 512), BF16),
            pltpu.VMEM((4, 3, 2, 24, 512), BF16),
            pltpu.VMEM((4, 4, 2, 2, 24, 512), BF16),
            pltpu.VMEM((4, 4, 2, 24, 512), BF16),
            pltpu.VMEM((8, 2, 128, 512), BF16),
            pltpu.VMEM((8, 2, 128, 512), BF16),
            pltpu.VMEM((2, 128, 512), BF16),
            pltpu.VMEM((768, 192), BF16),
            pltpu.VMEM((768, 192), BF16),
            pltpu.VMEM((768, 192), BF16),
            pltpu.VMEM((2, 768, 192), BF16),
            dma((4,)), dma((4,)), dma((4, 3)), dma((4, 3)), dma((4, 2)), dma((4, 2)),
            dma((4, 3)), dma((4, 3)), dma((8,)), dma((8,)), dma((3,)), dma((3,)), dma((2,)),
        ],
        compiler_params=pltpu.CompilerParams(
            collective_id=1, has_side_effects=True, vmem_limit_bytes=VMEM_LIMIT
        ),
    )(p, low, f, info, table)


def local(tokens, grad_out, route_weights, expert_ids, wg, wu, wd, ag, bg, au, bu, ad, bd):
    row = np.arange(48)
    table = (row // 24) * CAP + row % CAP + FAR * ((row // CAP) % 2)
    table = jnp.asarray(table.reshape(48, 1), F32)
    f, info = dispatch(tokens, grad_out, expert_ids.T, route_weights.T, table)
    p, low, gs, us, df = experts(f, wg, wu, wd, ag, bg, au, bu, ad, bd)
    out, gf, uf, ds = send_back(p, low, f, info, table)
    return out, gf, gs, uf, us, df, ds


def solution(mesh):
    specs = (
        P("expert", "tensor"), P("expert", "tensor"), P("expert", None), P("expert", None),
        P("expert", None, "tensor"), P("expert", None, "tensor"), P("expert", "tensor", None),
        P("expert", None, None), P("expert", None, "tensor"), P("expert", None, None),
        P("expert", None, "tensor"), P("expert", "tensor", None), P("expert", None, None),
    )
    outs = (
        P("expert", "tensor"), P("expert", "tensor", None), P("expert", None, "tensor"),
        P("expert", "tensor", None), P("expert", None, "tensor"), P("expert", "tensor", None),
        P("expert", None, "tensor"),
    )
    return jax.shard_map(local, mesh=mesh, in_specs=specs, out_specs=outs, check_vma=False)
```

time: 463 us -> 203 us (0.44); the launches traced: 454 us -> 202 us
  Pallas kernels: 0 us -> 184 us
  waiting for transfers between devices: 124 us -> 0 us
  blocking collectives: 113 us -> 0 us
  local copies, waits for them, and re-layouts: 127 us -> 17.1 us
  matrix products: 38.6 us -> 0 us
  starting transfers between devices: 19.3 us -> 0 us
  other arithmetic: 17.5 us -> 0 us
  between operations: 14.7 us -> 0.69 us
    pallas_call x0 -> x3, Pallas kernels: none -> 184 us  [the longest x1 86.6 us: dispatch(): pl.pallas_call(dispatch_kernel, name='dispatch', out_shape=(jax.ShapeDtyp...]
    all_to_all x2 -> x0, blocking collectives: 113 us -> none  [the longest x1 86.5 us: side_by_side(): lax.all_to_all(both, axis, split_axis=split_dim, concat_axis=concat_dim,...]
    all_gather x1 -> x0, waiting for transfers between devices: 73.7 us -> none  [sent_together(): result = lax.all_gather(both, axis, axis=dim, tiled=True)]
    reshape x6 -> x0, local copies, waits for them, and re-layouts: 46.3 us -> none  [the longest x2 18 us: local(): recv_grad.reshape(sources, local_experts, capacity, hidden_width)]
    dot_general x20 -> x0, matrix products: 38.6 us -> none  [the longest x1 8.46 us: local(): jnp.einsum('secf,edf->secd', joined_grad, joined_weight, preferred_elemen...]
    all_to_all x3 -> x0, waiting for transfers between devices: 37.6 us -> none  [the longest x2 23.9 us: from_everyone(): lax.all_to_all(jnp.broadcast_to(shard[None], (peers, *shard.shape)), axis...]
    unnamed x67 -> x20, local copies, waits for them, and re-layouts: 38.7 us -> 17.1 us
    all_to_all x3 -> x0, starting transfers between devices: 19.2 us -> none  [the longest x1 10.8 us: local(): lax.all_to_all(reduced.astype(jnp.bfloat16), 'expert', split_axis=0, conc...]
  transfers between devices with their start and end apart: 5 -> 0, of which waited for: 5 -> 0; matrix products, arithmetic and copies ran while one was open for 10% -> 0% of each run, Pallas kernels for 0% -> 0%
where the time goes in v1:
time: 203 us; the launch traced here: 202 us
  Pallas kernels  184 us (91%)
  local copies, waits for them, and re-layouts  17.1 us (8%)
    pallas_call x1, Pallas kernels, dispatch(): pl.pallas_call(dispatch_kernel, name='dispatch', out_shape=(jax.ShapeDtyp...  86.6 us
    pallas_call x1, Pallas kernels, send_back(): pl.pallas_call(return_kernel, name='send_back', out_shape=(jax.ShapeDtype...  63.3 us
    pallas_call x1, Pallas kernels, experts(): pl.pallas_call(expert_kernel, name='experts', out_shape=(jax.ShapeDtypeSt...  33.9 us
    unnamed x20, local copies, waits for them, and re-layouts  17.1 us

profile of v1, /device:TPU:24, one launch (start us, length us, event | category | flops | bytes accessed | tf_op | source)
XLA Modules:
  0.0 201.6 jit_solution(17984781353112415271)
XLA Ops:
  0.6 0.0 copy-start.2
  0.6 0.0 copy-start
  0.7 1.7 copy.25.ad_ref
  2.4 2.4 %copy.23.ag_ref = bf16[2,2048,64]{2,1,0:T(8,128)(2,1)} copy(bf16[2,2048,64]{1,2,0:T(8,128)(2,1)} %param.21) | data formatting | bytes 1048576 | tf_op args[7]
  4.8 0.0 copy-done.2
  4.8 1.3 copy.24.au_ref
  6.1 0.0 copy-done
  6.1 0.0 copy-start.1
  6.1 2.4 %copy.21.wg_ref = bf16[2,2048,192]{2,1,0:T(8,128)(2,1)} copy(bf16[2,2048,192]{1,2,0:T(8,128)(2,1)S(1)} %copy-done) | data formatting | bytes 3145728 | tf_op args[4]
  8.5 0.0 copy-done.1
  8.5 2.4 %copy.22.wu_ref = bf16[2,2048,192]{2,1,0:T(8,128)(2,1)} copy(bf16[2,2048,192]{1,2,0:T(8,128)(2,1)S(1)} %copy-done.1) | data formatting | bytes 3145728 | tf_op args[5]
  10.9 86.6 %dispatch.1 = (bf16[2,2,2,4,2,4,24,1024]{7,6,5,4,3,2,1,0:T(8,128)(2,1)}, f32[8,16,128]{2,1,0:T(8,128)}) custom-call(bf16[128,512]{1,0:T(8,128)(2,1)} %tok_ref.1, bf16[128,512]{1,0:T(8,128)(2,1)} %grad_ref.1, s32[8,128]{1,0:T(8,128)} %bitcast.2, f32[8,128]{1,0:T(8,128)} %bitcast.3, f32[48,1]{1,0:T(8,128)} %constant.2.clone.table_ref), custom_call_target="tpu_custom_call" | custom-call | tf_op jit(solution)/shard_map/dispatch/pallas_call | solution.py:270
  97.5 33.9 %experts.1 = (bf16[2,2,2,4,2,4,24,512]{7,6,5,4,3,2,1,0:T(8,128)(2,1)}, bf16[2,768,192]{2,1,0:T(8,128)(2,1)}, f32[2,64,192]{2,1,0:T(8,128)}, f32[2,64,192]{2,1,0:T(8,128)}, f32[2,192,64]{2,1,0:T(8,128)}) custom-call(bf16[2,2,2,4,2,4,24,1024]{7,6,5,4,3,2,1,0:T(8,128)(2,1)} %get-tuple-element.18.f_ref, bf16[2,2048,192]{2,1,0:T(8,128)(2,1)} %copy.21.wg_ref, ...), custom_call_target="tpu_custom_call" | custom-call | tf_op jit(solution)/shard_map/experts/pallas_call | solution.py:369
  131.4 0.0 copy-start.4
  131.4 63.3 %send_back.1 = (bf16[128,512]{1,0:T(8,128)(2,1)}, f32[2,512,64]{2,1,0:T(8,128)}, f32[2,512,64]{2,1,0:T(8,128)}, f32[2,64,512]{2,1,0:T(8,128)}) custom-call(bf16[2,2,2,4,2,4,24,512]{7,6,5,4,3,2,1,0:T(8,128)(2,1)} %get-tuple-element.19.p_ref, bf16[2,768,192]{2,1,0:T(8,128)(2,1)} %get-tuple-element.20.low_ref, ...), custom_call_target="tpu_custom_call" | custom-call | tf_op jit(solution)/shard_map/send_back/pallas_call | solution.py:573
  194.7 0.0 copy-start.3
  194.7 0.0 copy-done.4
  194.7 0.8 copy.28
  195.5 1.9 copy.26
  197.4 1.9 copy.27
  199.4 1.6 copy.31
  200.9 0.0 copy-done.3
  200.9 0.7 copy.32
Async XLA Ops:
  0.6 4.1 %copy-start.2 = (bf16[2,2048,64]{1,2,0:T(8,128)(2,1)S(1)}, bf16[2,2048,64]{1,2,0:T(8,128)(2,1)}, u32[]{:S(2)}) copy-start(bf16[2,2048,64]{1,2,0:T(8,128)(2,1)} %param.23) | copy-start | bytes 1572868
  0.6 5.5 %copy-start = (bf16[2,2048,192]{1,2,0:T(8,128)(2,1)S(1)}, bf16[2,2048,192]{1,2,0:T(8,128)(2,1)}, u32[]{:S(2)}) copy-start(bf16[2,2048,192]{1,2,0:T(8,128)(2,1)} %param.18) | copy-start | bytes 4718596
  6.1 2.4 %copy-start.1 = (bf16[2,2048,192]{1,2,0:T(8,128)(2,1)S(1)}, bf16[2,2048,192]{1,2,0:T(8,128)(2,1)}, u32[]{:S(2)}) copy-start(bf16[2,2048,192]{1,2,0:T(8,128)(2,1)} %param.19) | copy-start | bytes 4718596
  131.4 63.3 %copy-start.4 = (f32[2,192,64]{2,1,0:T(8,128)S(1)}, f32[2,192,64]{2,1,0:T(8,128)}, u32[]{:S(2)}) copy-start(f32[2,192,64]{2,1,0:T(8,128)} %get-tuple-element.34) | copy-start | bytes 294916
  194.7 6.2 %copy-start.3 = (f32[2,64,512]{2,1,0:T(8,128)S(1)}, f32[2,64,512]{2,1,0:T(8,128)}, u32[]{:S(2)}) copy-start(f32[2,64,512]{2,1,0:T(8,128)} %get-tuple-element.49) | copy-start | bytes 786436

commit v2 on v0

v2 whole, which is shorter than its diff:
```python
import functools

import jax
import jax.numpy as jnp
import numpy as np
from jax import lax
from jax.experimental import pallas as pl
from jax.experimental.pallas import tpu as pltpu
from jax.sharding import PartitionSpec as P

MESH = pl.DeviceIdType.MESH
F32 = jnp.float32
BF16 = jnp.bfloat16
PAIRS = ((0, 1), (-1, 2), (-3, 4), (-2, 3))
CAP = 12
FAR = 4096.0
VMEM_LIMIT = 67043328


def place():
    expert = lax.axis_index("expert")
    tensor = lax.axis_index("tensor")
    y = expert % 4
    z = (expert // 4) % 8
    xl = expert // 32
    xh = tensor // 2
    core = tensor % 2
    return xl, xh, y, z, core


def device(xl, xh, y, z, core):
    return (xl * 32 + z * 4 + y, xh * 2 + core)


def rem_copy(src, dst, send, recv, target):
    return pltpu.make_async_remote_copy(
        src_ref=src, dst_ref=dst, send_sem=send, recv_sem=recv,
        device_id=target, device_id_type=MESH,
    )


def side(xl, xh, step):
    x = (xh * 2 + xl + step) % 4
    return x % 2, x // 2


def greet(targets):
    barrier = pltpu.get_barrier_semaphore()
    for target in targets:
        pl.semaphore_signal(barrier, inc=1, device_id=target, device_id_type=MESH)
    pl.semaphore_wait(barrier, len(targets))


def nt(a, b):
    return lax.dot_general(a, b, (((1,), (1,)), ((), ())), preferred_element_type=F32)


def tn(a, b):
    return lax.dot_general(a, b, (((0,), (0,)), ((), ())), preferred_element_type=F32)


def nn(a, b):
    return jnp.dot(a, b, preferred_element_type=F32)


def one_hot(ids, positions, weights):
    hot = jnp.zeros((96, 256), F32)
    weight = jnp.zeros((96, 256), F32)
    for k in range(8):
        match = ids == positions[k : k + 1]
        hot = jnp.where(match, 1.0, hot)
        if weights is not None:
            weight = jnp.where(match, weights[k : k + 1], weight)
    if weights is None:
        return hot.astype(BF16)
    return hot.astype(BF16), jnp.sum(weight, axis=1, keepdims=True)


def kernel(
    tok_ref, grad_ref, ids_ref, rw_ref, table_ref,
    wg_hbm, wu_hbm, wd_hbm, ag_hbm, bg_hbm, au_hbm, bu_hbm, ad_hbm, bd_hbm,
    out_ref, gf_ref, gs_ref, uf_ref, us_ref, df_ref, ds_ref,
    wg_ref, wu_ref, wd_ref, ag_ref, bg_ref, au_ref, bu_ref, ad_ref, bd_ref, w_sem,
    info_ref, zb, stage_same, stage_diff, relay, f_ref,
    p_ref, r1, cps, cpx, xr, xs_stage, ys, yd, t_ref, zs, zr, fin, low_ref, rl, ls, rl2, tl,
    info_send, info_recv, swap_sem, ring_send, ring_recv,
    same_send, same_recv, diff_send, diff_recv, x_send, x_recv, core_send, core_recv,
    pc_send, pc_recv, ps_send, ps_recv, px_send, px_recv, pd_send, pd_recv,
    z_send, z_recv, l_send, l_recv, f_sem,
):
    xl, xh, y, z, core = place()
    here = functools.partial(device, xl, xh)
    z_others = [here(y, (z + d) % 8, core) for d in range(1, 8)]
    y_others = [here((y + j) % 4, z, core) for j in range(1, 4)]
    x_sides = [device(*side(xl, xh, s), y, z, core) for s in (1, 3)]
    x_far = device(xl, 1 - xh, y, z, core)
    partner = here(y, z, 1 - core)
    down, up = here(y, (z + 7) % 8, core), here(y, (z + 1) % 8, core)

    loads = []
    for n, (src, dst) in enumerate((
        (wg_hbm, wg_ref), (wu_hbm, wu_ref), (wd_hbm, wd_ref), (ag_hbm, ag_ref), (bg_hbm, bg_ref),
        (au_hbm, au_ref), (bu_hbm, bu_ref), (ad_hbm, ad_ref), (bd_hbm, bd_ref),
    )):
        load = pltpu.make_async_copy(src, dst, w_sem.at[n])
        load.start()
        loads.append(load)

    zb[0, 0, :, 0:512] = tok_ref[...]
    zb[0, 0, :, 512:1024] = grad_ref[...]

    ids = ids_ref[...]
    numbers = lax.broadcasted_iota(jnp.int32, (128, 128), 0)
    picked = jnp.zeros((128, 128), F32)
    for k in range(8):
        picked = jnp.where(ids[k : k + 1] == numbers, 1.0, picked)
    later = lax.broadcasted_iota(jnp.int32, (128, 128), 1) > numbers
    before = nn(picked.astype(BF16), jnp.where(later, 1.0, 0.0).astype(BF16))
    for k in range(8):
        slot = jnp.sum(jnp.where(ids[k : k + 1] == numbers, before, 0.0), axis=0, keepdims=True)
        info_ref[0, k : k + 1, :] = ids[k : k + 1].astype(F32) * CAP + slot
    info_ref[0, 8:16, :] = rw_ref[...]

    greet(z_others + y_others + x_sides + [x_far, partner])

    swap = rem_copy(zb.at[0, 0], zb.at[0, 1], swap_sem.at[0], swap_sem.at[1], x_far)
    swap.start()

    def ring(direction, h, chunk):
        if direction == 0:
            src, dst = (h - 1) % 8, h % 8
        else:
            src, dst = (1 - h) % 8, (-h) % 8
        n = (h - 1) * 2 + chunk
        return rem_copy(
            zb.at[src, chunk], zb.at[dst, chunk],
            ring_send.at[direction, n], ring_recv.at[direction, n],
            down if direction == 0 else up,
        )

    ring(0, 1, 0).start()
    ring(1, 1, 0).start()
    infos = []
    for d in range(1, 8):
        copy = rem_copy(
            info_ref.at[0], info_ref.at[(8 - d) % 8], info_send.at[d - 1], info_recv.at[d - 1],
            z_others[d - 1],
        )
        copy.start()
        infos.append(copy)
    swap.wait_recv()
    ring(0, 1, 1).start()
    ring(1, 1, 1).start()
    for copy in infos:
        copy.wait_recv()

    def advance(h):
        for chunk in (0, 1):
            for direction in (0, 1):
                if h == 4 and chunk != direction:
                    continue
                ring(direction, h, chunk).wait_recv()
                if h < 3 or (h == 3 and chunk == direction):
                    ring(direction, h + 1, chunk).start()

    def same_copy(p, e, j):
        return rem_copy(
            stage_same.at[p, e, j - 1], f_ref.at[core, :, e, p, xl, y],
            same_send.at[p, e, j - 1], same_recv.at[p, e, j - 1], here((y + j) % 4, z, core),
        )

    def diff_copy(p, e, j):
        return rem_copy(
            stage_diff.at[p, e, j - 1], relay.at[p, e, y],
            diff_send.at[p, e, j - 1], diff_recv.at[p, e, j - 1], here((y + j) % 4, z, core),
        )

    def x_copy(p, e, s):
        return rem_copy(
            relay.at[p, e], f_ref.at[core, xh, e, p, xl],
            x_send.at[p, e, s], x_recv.at[p, e, s], x_sides[s],
        )

    def core_copy(p, e, part):
        if part == 0:
            piece = f_ref.at[core, :, e, p, xl]
        else:
            from_xl, from_xh = side(xl, xh, (1, 3)[part - 1])
            piece = f_ref.at[core, from_xh, e, p, from_xl]
        return rem_copy(piece, piece, core_send.at[p, e, part], core_recv.at[p, e, part], partner)

    def pc_copy(p, e):
        return rem_copy(
            p_ref.at[1 - core, :, e, p], r1.at[:, e, p], pc_send.at[p, e], pc_recv.at[p, e], partner
        )

    def ps_copy(p, e, j):
        return rem_copy(
            cps.at[p, e, j - 1], ys.at[p, :, e, y], ps_send.at[p, e, j - 1], ps_recv.at[p, e, j - 1],
            here((y + j) % 4, z, core),
        )

    def pd_copy(p, e, j):
        return rem_copy(
            xs_stage.at[p, e, j - 1], yd.at[p, e, y], pd_send.at[p, e, j - 1], pd_recv.at[p, e, j - 1],
            here((y + j) % 4, z, core),
        )

    def px_copy(p, e, s):
        _, to_xh = side(xl, xh, (1, 3)[s])
        return rem_copy(
            cpx.at[p, e, to_xh], xr.at[p, e, xh], px_send.at[p, e, s], px_recv.at[p, e, s], x_sides[s]
        )

    def z_copy(direction, h, chunk):
        n = direction * 4 + h - 1
        return rem_copy(
            zs.at[n, chunk], zr.at[n, chunk], z_send.at[n, chunk], z_recv.at[n, chunk],
            up if direction == 0 else down,
        )

    low_core = rem_copy(low_ref.at[1 - core], rl, l_send.at[0], l_recv.at[0], partner)
    low_far = rem_copy(ls, rl2, l_send.at[1], l_recv.at[1], x_far)
    low_back = rem_copy(tl.at[core], tl.at[core], l_send.at[2], l_recv.at[2], partner)

    table = table_ref[...]

    def row_ids(target_xl, e, first):
        return jnp.concatenate(
            [
                table + ((target_xl * 64 + z * 8 + ((first + j) % 4) * 2 + e) * CAP).astype(F32)
                for j in range(4)
            ],
            axis=0,
        )

    def pair_info(p, weights):
        a, b = PAIRS[p][0] % 8, PAIRS[p][1] % 8
        positions = jnp.concatenate([info_ref[a, 0:8], info_ref[b, 0:8] + FAR], axis=1)
        if not weights:
            return positions, None
        return positions, jnp.concatenate([info_ref[a, 8:16], info_ref[b, 8:16]], axis=1)

    def select(p):
        a, b = PAIRS[p][0] % 8, PAIRS[p][1] % 8
        positions, weights = pair_info(p, True)
        own = jnp.concatenate([zb[a, 0], zb[b, 0]], axis=0)
        other = jnp.concatenate([zb[a, 1], zb[b, 1]], axis=0)

        def rows_of(hot, weight, x):
            rows = nn(hot, x)
            taken = rows[:, 0:512].astype(BF16)
            scaled = (rows[:, 512:1024] * weight).astype(BF16)
            return jnp.concatenate([taken, scaled], axis=1).reshape(4, 24, 1024)

        for e in (0, 1):
            hot, weight = one_hot(row_ids(1 - xl, e, y), positions, weights)
            rows = rows_of(hot, weight, own)
            relay[p, e, y] = rows[0]
            for j in range(1, 4):
                stage_diff[p, e, j - 1] = rows[j]
                diff_copy(p, e, j).start()
            hot, weight = one_hot(row_ids(xl, e, y), positions, weights)
            rows = rows_of(hot, weight, own)
            rows_b = rows_of(hot, weight, other)
            f_ref[core, xh, e, p, xl, y] = rows[0]
            f_ref[core, 1 - xh, e, p, xl, y] = rows_b[0]
            for j in range(1, 4):
                stage_same[p, e, j - 1, xh] = rows[j]
                stage_same[p, e, j - 1, 1 - xh] = rows_b[j]
                same_copy(p, e, j).start()

    def forward(u):
        p, e = u // 2, u % 2
        for j in range(1, 4):
            diff_copy(p, e, j).wait_recv()
        x_copy(p, e, 0).start()
        x_copy(p, e, 1).start()
        for j in range(1, 4):
            same_copy(p, e, j).wait_recv()
        core_copy(p, e, 0).start()

    def gather(u):
        p, e = u // 2, u % 2
        for s in (0, 1):
            x_copy(p, e, 1 - s).wait_recv()
            core_copy(p, e, 1 + s).start()

    def compute(u):
        p, e = u // 2, u % 2
        for part in range(3):
            core_copy(p, e, part).wait_recv()

        def take(cq, qh, lo):
            return f_ref[cq, qh, e, p, :, :, :, lo : lo + 512].reshape(192, 512)

        x = jnp.concatenate([take(0, 0, 0), take(1, 0, 0), take(0, 1, 0), take(1, 1, 0)], axis=1)
        gate_in = jnp.concatenate([wg_ref[e], ag_ref[e]], axis=0)
        up_in = jnp.concatenate([wu_ref[e], au_ref[e]], axis=0)
        down_in = jnp.concatenate([wd_ref[e], bd_ref[e]], axis=0)
        gate = nt(x, gate_in)
        lg = gate[:, 192:256].astype(BF16)
        gate = gate[:, 0:192] + 0.5 * nn(lg, bg_ref[e])
        up_part = nt(x, up_in)
        lu = up_part[:, 192:256].astype(BF16)
        up_part = up_part[:, 0:192] + 0.5 * nn(lu, bu_ref[e])
        sigma = jax.nn.sigmoid(gate)
        active = gate * sigma
        hidden = (active * up_part).astype(BF16)
        down_part = nt(hidden, ad_ref[e]).astype(BF16)
        g = jnp.concatenate(
            [take(0, 0, 512), take(1, 0, 512), take(0, 1, 512), take(1, 1, 512)], axis=1
        )
        gh = nt(g, down_in)
        back = gh[:, 192:256].astype(BF16)
        gh = gh[:, 0:192] + 0.5 * nn(back, ad_ref[e])
        gg = (gh * up_part * sigma * (1.0 + gate * (1.0 - sigma))).astype(BF16)
        gu = (gh * active).astype(BF16)
        gp = nt(gg, bg_ref[e]).astype(BF16)
        upp = nt(gu, bu_ref[e]).astype(BF16)
        left = jnp.concatenate([gg, gp * 0.5], axis=1)
        right = jnp.concatenate([gu, upp * 0.5], axis=1)
        for q in range(4):
            cols = slice(q * 512, q * 512 + 512)
            part = nn(left, gate_in[:, cols]) + nn(right, up_in[:, cols])
            p_ref[q % 2, q // 2, e, p] = part.astype(BF16).reshape(2, 4, 24, 512)
        pc_copy(p, e).start()
        rows = slice(p * 192, p * 192 + 192)
        low_ref[e, rows, 0:64] = down_part
        low_ref[e, rows, 64:128] = gp
        low_ref[e, rows, 128:192] = upp
        for ref, value in ((gs_ref, tn(lg, gg)), (us_ref, tn(lu, gu)), (df_ref, tn(back, hidden))):
            if p == 0:
                ref[e] = 0.5 * value
            else:
                ref[e] += 0.5 * value

    def chip_sum(u):
        p, e = u // 2, u % 2
        pc_copy(p, e).wait_recv()
        for qh in (0, 1):
            mine = p_ref[core, qh, e, p, 1 - xl].astype(F32)
            cpx[p, e, qh] = (mine + r1[qh, e, p, 1 - xl].astype(F32)).astype(BF16)
        px_copy(p, e, 0).start()
        px_copy(p, e, 1).start()
        for j in range(4):
            to = (y + j) % 4
            mine = p_ref[core, :, e, p, xl, to].astype(F32)
            total = (mine + r1[:, e, p, xl, to].astype(F32)).astype(BF16)
            if j == 0:
                ys[p, :, e, y] = total
            else:
                cps[p, e, j - 1] = total
                ps_copy(p, e, j).start()

    def x_sum(u):
        p, e = u // 2, u % 2
        px_copy(p, e, 0).wait_recv()
        px_copy(p, e, 1).wait_recv()
        for j in range(4):
            to = (y + j) % 4
            total = (xr[p, e, 0, to].astype(F32) + xr[p, e, 1, to].astype(F32)).astype(BF16)
            if j == 0:
                yd[p, e, y] = total
            else:
                xs_stage[p, e, j - 1] = total
                pd_copy(p, e, j).start()

    def combine(p):
        positions, _ = pair_info(p, False)
        hot_same = jnp.concatenate(
            [one_hot(row_ids(xl, e, 0), positions, None) for e in (0, 1)], axis=0
        )
        hot_diff = jnp.concatenate(
            [one_hot(row_ids(1 - xl, e, 0), positions, None) for e in (0, 1)], axis=0
        )
        for e in (0, 1):
            for j in range(1, 4):
                ps_copy(p, e, j).wait_recv()
                pd_copy(p, e, j).wait_recv()
        t_ref[p, 1] = tn(hot_same, ys[p, 1 - xh].reshape(192, 512))
        t_ref[p, 0] = tn(hot_same, ys[p, xh].reshape(192, 512)) + tn(hot_diff, yd[p].reshape(192, 512))

    held = {d: (p, i) for p in range(4) for i, d in enumerate(PAIRS[p])}

    def part_of(distance, chunk):
        p, i = held[distance]
        return t_ref[p, chunk, i * 128 : i * 128 + 128]

    def z_hop(direction, h, chunk):
        if h == 1 and chunk != direction:
            return
        n = direction * 4 + h - 1
        distance = 5 - h
        value = part_of(distance if direction == 0 or h == 1 else -distance, chunk)
        if h > 2 or (h == 2 and chunk == direction):
            z_copy(direction, h - 1, chunk).wait_recv()
            value = value + zr[n - 1, chunk].astype(F32)
        zs[n, chunk] = value.astype(BF16)
        z_copy(direction, h, chunk).start()

    advance(1)
    select(0)
    forward(0)
    advance(2)
    select(1)
    gather(0)
    forward(1)
    for load in loads:
        load.wait()
    compute(0)
    advance(3)
    gather(1)
    forward(2)
    chip_sum(0)
    compute(1)
    x_sum(0)
    advance(4)
    select(2)
    select(3)
    gather(2)
    forward(3)
    for u in range(1, 7):
        chip_sum(u)
        compute(u + 1)
        x_sum(u)
        if u == 4:
            combine(0)
        if u == 6:
            combine(1)
        if u + 2 < 8:
            gather(u + 2)
        if u + 3 < 8:
            forward(u + 3)
    low_core.start()
    chip_sum(7)
    low_core.wait_recv()
    ls[...] = (low_ref[core].astype(F32) + rl[...].astype(F32)).astype(BF16)
    low_far.start()
    combine(2)
    z_hop(0, 1, 0)
    z_hop(1, 1, 1)
    x_sum(7)
    combine(3)
    for chunk in (1, 0):
        z_hop(0, 2, chunk)
        z_hop(1, 2, chunk)
    low_far.wait_recv()
    tl[core] = (ls[...].astype(F32) + rl2[...].astype(F32)).astype(BF16)
    low_back.start()
    for chunk in (1, 0):
        z_hop(0, 3, chunk)
        z_hop(1, 3, chunk)

    low_back.wait_recv()

    def adapters(e):
        quarter = f_ref[core, xh, e].reshape(768, 1024)
        total = tl[e]
        both = 0.5 * tn(total[:, 64:192], quarter[:, 0:512])
        gf_ref[e] = both[0:64]
        uf_ref[e] = both[64:128]
        ds_ref[e] = 0.5 * tn(total[:, 0:64], quarter[:, 512:1024])

    adapters(0)
    for chunk in (1, 0):
        z_hop(0, 4, chunk)
        z_hop(1, 4, chunk)
    adapters(1)

    def home(chunk):
        z_copy(0, 4, chunk).wait_recv()
        z_copy(1, 4, chunk).wait_recv()
        return part_of(0, chunk) + zr[3, chunk].astype(F32) + zr[7, chunk].astype(F32)

    fin[0] = home(1).astype(BF16)
    last = rem_copy(fin.at[0], fin.at[1], f_sem.at[0], f_sem.at[1], x_far)
    last.start()
    mine = home(0)
    last.wait_recv()
    out_ref[...] = (mine + fin[1].astype(F32)).astype(BF16)

    last.wait_send()
    swap.wait_send()
    for copy in infos:
        copy.wait_send()
    low_core.wait_send()
    low_far.wait_send()
    low_back.wait_send()
    for direction in (0, 1):
        for h in range(1, 5):
            for chunk in (0, 1):
                if h < 4 or chunk == direction:
                    ring(direction, h, chunk).wait_send()
                if h > 1 or chunk == direction:
                    z_copy(direction, h, chunk).wait_send()
    for p in range(4):
        for e in (0, 1):
            pc_copy(p, e).wait_send()
            for s in (0, 1):
                x_copy(p, e, s).wait_send()
                px_copy(p, e, s).wait_send()
            for n in range(3):
                same_copy(p, e, n + 1).wait_send()
                diff_copy(p, e, n + 1).wait_send()
                ps_copy(p, e, n + 1).wait_send()
                pd_copy(p, e, n + 1).wait_send()
                core_copy(p, e, n).wait_send()


def step(tokens, grad_out, ids, weights, table, *frozen):
    vmem = pl.BlockSpec(memory_space=pltpu.VMEM)
    hbm = pl.BlockSpec(memory_space=pl.ANY)
    dma = pltpu.SemaphoreType.DMA

    def buf(*shape):
        return pltpu.VMEM(shape, BF16)

    return pl.pallas_call(
        kernel,
        name="experts",
        out_shape=(
            jax.ShapeDtypeStruct((128, 512), BF16),
            jax.ShapeDtypeStruct((2, 64, 512), F32),
            jax.ShapeDtypeStruct((2, 64, 192), F32),
            jax.ShapeDtypeStruct((2, 64, 512), F32),
            jax.ShapeDtypeStruct((2, 64, 192), F32),
            jax.ShapeDtypeStruct((2, 64, 192), F32),
            jax.ShapeDtypeStruct((2, 64, 512), F32),
        ),
        in_specs=[vmem] * 5 + [hbm] * 9,
        out_specs=(vmem,) * 7,
        scratch_shapes=[buf(*w.shape) for w in frozen] + [
            dma((9,)),
            pltpu.VMEM((8, 16, 128), F32),
            buf(8, 2, 128, 1024),
            buf(4, 2, 3, 2, 24, 1024),
            buf(4, 2, 3, 24, 1024),
            buf(4, 2, 4, 24, 1024),
            buf(2, 2, 2, 4, 2, 4, 24, 1024),
            buf(2, 2, 2, 4, 2, 4, 24, 512),
            buf(2, 2, 4, 2, 4, 24, 512),
            buf(4, 2, 3, 2, 24, 512),
            buf(4, 2, 2, 4, 24, 512),
            buf(4, 2, 2, 4, 24, 512),
            buf(4, 2, 3, 24, 512),
            buf(4, 2, 2, 4, 24, 512),
            buf(4, 2, 4, 24, 512),
            pltpu.VMEM((4, 2, 256, 512), F32),
            buf(8, 2, 128, 512),
            buf(8, 2, 128, 512),
            buf(2, 128, 512),
            buf(2, 768, 192),
            buf(768, 192),
            buf(768, 192),
            buf(768, 192),
            buf(2, 768, 192),
            dma((7,)), dma((7,)), dma((2,)), dma((2, 8)), dma((2, 8)),
            dma((4, 2, 3)), dma((4, 2, 3)), dma((4, 2, 3)), dma((4, 2, 3)),
            dma((4, 2, 2)), dma((4, 2, 2)), dma((4, 2, 3)), dma((4, 2, 3)),
            dma((4, 2)), dma((4, 2)), dma((4, 2, 3)), dma((4, 2, 3)),
            dma((4, 2, 2)), dma((4, 2, 2)), dma((4, 2, 3)), dma((4, 2, 3)),
            dma((8, 2)), dma((8, 2)), dma((3,)), dma((3,)), dma((2,)),
        ],
        compiler_params=pltpu.CompilerParams(
            collective_id=0, has_side_effects=True, vmem_limit_bytes=VMEM_LIMIT
        ),
    )(tokens, grad_out, ids, weights, table, *frozen)


def finish_kernel(*refs):
    for src, dst in zip(refs[:7], refs[7:]):
        dst[...] = src[...]


def finish(outs):
    vmem = pl.BlockSpec(memory_space=pltpu.VMEM)
    return pl.pallas_call(
        finish_kernel,
        name="finish",
        out_shape=tuple(jax.ShapeDtypeStruct(o.shape, o.dtype) for o in outs),
        in_specs=[vmem] * 7,
        out_specs=(vmem,) * 7,
    )(*outs)


def local(tokens, grad_out, route_weights, expert_ids, wg, wu, wd, ag, bg, au, bu, ad, bd):
    row = np.arange(24)
    table = row % CAP + FAR * (row // CAP)
    table = jnp.asarray(table.reshape(24, 1), F32)
    wg, wu, ag, au, ad = [jnp.swapaxes(w, 1, 2) for w in (wg, wu, ag, au, ad)]
    outs = step(
        tokens, grad_out, expert_ids.T, route_weights.T, table, wg, wu, wd, ag, bg, au, bu, ad, bd
    )
    out, gf, gs, uf, us, df, ds = finish(outs)
    gf, uf, df = [jnp.swapaxes(w, 1, 2) for w in (gf, uf, df)]
    return out, gf, gs, uf, us, df, ds


def solution(mesh):
    specs = (
        P("expert", "tensor"), P("expert", "tensor"), P("expert", None), P("expert", None),
        P("expert", None, "tensor"), P("expert", None, "tensor"), P("expert", "tensor", None),
        P("expert", None, None), P("expert", None, "tensor"), P("expert", None, None),
        P("expert", None, "tensor"), P("expert", "tensor", None), P("expert", None, None),
    )
    outs = (
        P("expert", "tensor"), P("expert", "tensor", None), P("expert", None, "tensor"),
        P("expert", "tensor", None), P("expert", None, "tensor"), P("expert", "tensor", None),
        P("expert", None, "tensor"),
    )
    return jax.shard_map(local, mesh=mesh, in_specs=specs, out_specs=outs, check_vma=False)
```

time: 463 us -> 144 us (0.31); the launches traced: 454 us -> 141 us
  Pallas kernels: 0 us -> 141 us
  local copies, waits for them, and re-layouts: 127 us -> 0 us
  waiting for transfers between devices: 124 us -> 0 us
  blocking collectives: 113 us -> 0 us
  matrix products: 38.6 us -> 0 us
  starting transfers between devices: 19.3 us -> 0 us
  other arithmetic: 17.5 us -> 0 us
  between operations: 14.7 us -> 0.65 us
    pallas_call x0 -> x2, Pallas kernels: none -> 141 us  [the longest x1 138 us: step(): pl.pallas_call(kernel, name='experts', out_shape=(jax.ShapeDtypeStruct((1...]
    all_to_all x2 -> x0, blocking collectives: 113 us -> none  [the longest x1 86.5 us: side_by_side(): lax.all_to_all(both, axis, split_axis=split_dim, concat_axis=concat_dim,...]
    all_gather x1 -> x0, waiting for transfers between devices: 73.7 us -> none  [sent_together(): result = lax.all_gather(both, axis, axis=dim, tiled=True)]
    reshape x6 -> x0, local copies, waits for them, and re-layouts: 46.3 us -> none  [the longest x2 18 us: local(): recv_grad.reshape(sources, local_experts, capacity, hidden_width)]
    unnamed x67 -> x0, local copies, waits for them, and re-layouts: 38.7 us -> none
    dot_general x20 -> x0, matrix products: 38.6 us -> none  [the longest x1 8.46 us: local(): jnp.einsum('secf,edf->secd', joined_grad, joined_weight, preferred_elemen...]
    all_to_all x3 -> x0, waiting for transfers between devices: 37.6 us -> none  [the longest x2 23.9 us: from_everyone(): lax.all_to_all(jnp.broadcast_to(shard[None], (peers, *shard.shape)), axis...]
    all_to_all x3 -> x0, starting transfers between devices: 19.2 us -> none  [the longest x1 10.8 us: local(): lax.all_to_all(reduced.astype(jnp.bfloat16), 'expert', split_axis=0, conc...]
  transfers between devices with their start and end apart: 5 -> 0, of which waited for: 5 -> 0; matrix products, arithmetic and copies ran while one was open for 10% -> 0% of each run, Pallas kernels for 0% -> 0%
where the time goes in v2:
time: 144 us; the launch traced here: 141 us
  Pallas kernels  141 us (98%)
    pallas_call x1, Pallas kernels, step(): pl.pallas_call(kernel, name='experts', out_shape=(jax.ShapeDtypeStruct((1...  138 us

profile of v2, /device:TPU:24, one launch (start us, length us, event | category | flops | bytes accessed | tf_op | source)
XLA Modules:
  0.0 141.4 jit_solution(9649781673590705411)
XLA Ops:
  0.6 138.4 %experts.1 = (bf16[128,512]{1,0:T(8,128)(2,1)}, f32[2,64,512]{2,1,0:T(8,128)}, f32[2,64,192]{2,1,0:T(8,128)}, f32[2,64,512]{2,1,0:T(8,128)}, f32[2,64,192]{2,1,0...) custom-call(bf16[128,512]{1,0:T(8,128)(2,1)} %tok_ref.1, bf16[128,512]{1,0:T(8,128)(2,1)} %grad_ref.1, ...), custom_call_target="tpu_custom_call" | custom-call | tf_op jit(solution)/shard_map/experts/pallas_call | solution.py:519
  139.1 2.3 %finish.1 = (bf16[128,512]{1,0:T(8,128)(2,1)}, f32[2,64,512]{2,1,0:T(8,128)}, f32[2,64,192]{2,1,0:T(8,128)}, f32[2,64,512]{2,1,0:T(8,128)}, f32[2,64,192]{2,1,0:...) custom-call(bf16[128,512]{1,0:T(8,128)(2,1)} %get-tuple-element.21.refs_0_, ...), custom_call_target="tpu_custom_call" | custom-call | tf_op jit(solution)/shard_map/finish/pallas_call | solution.py:578

commit v3 on v2

v3 whole, which is shorter than its diff:
```python
import functools

import jax
import jax.numpy as jnp
import numpy as np
from jax import lax
from jax.experimental import pallas as pl
from jax.experimental.pallas import tpu as pltpu
from jax.sharding import PartitionSpec as P

MESH = pl.DeviceIdType.MESH
F32 = jnp.float32
BF16 = jnp.bfloat16
PAIRS = ((0, 1), (-1, 2), (-2, 3), (-3, 4))
CAP = 12
FAR = 4096.0
VMEM_LIMIT = 67043328


def place():
    expert = lax.axis_index("expert")
    tensor = lax.axis_index("tensor")
    y = expert % 4
    z = (expert // 4) % 8
    xl = expert // 32
    xh = tensor // 2
    core = tensor % 2
    return xl, xh, y, z, core


def device(xl, xh, y, z, core):
    return (xl * 32 + z * 4 + y, xh * 2 + core)


def rem_copy(src, dst, send, recv, target):
    return pltpu.make_async_remote_copy(
        src_ref=src, dst_ref=dst, send_sem=send, recv_sem=recv,
        device_id=target, device_id_type=MESH,
    )


def drain(ref, sem):
    pltpu.make_async_copy(ref, ref, sem).wait()


def side(xl, xh, step):
    x = (xh * 2 + xl + step) % 4
    return x % 2, x // 2


def greet(targets):
    barrier = pltpu.get_barrier_semaphore()
    for target in targets:
        pl.semaphore_signal(barrier, inc=1, device_id=target, device_id_type=MESH)
    pl.semaphore_wait(barrier, len(targets))


def nt(a, b):
    return lax.dot_general(a, b, (((1,), (1,)), ((), ())), preferred_element_type=F32)


def tn(a, b):
    return lax.dot_general(a, b, (((0,), (0,)), ((), ())), preferred_element_type=F32)


def nn(a, b):
    return jnp.dot(a, b, preferred_element_type=F32)


def one_hot(ids, positions, weights):
    hot = jnp.zeros((96, 256), F32)
    weight = jnp.zeros((96, 256), F32)
    for k in range(8):
        match = ids == positions[k : k + 1]
        hot = jnp.where(match, 1.0, hot)
        if weights is not None:
            weight = jnp.where(match, weights[k : k + 1], weight)
    if weights is None:
        return hot.astype(BF16)
    return hot.astype(BF16), jnp.sum(weight, axis=1, keepdims=True)


def kernel(
    tok_ref, grad_ref, ids_ref, rw_ref, table_ref,
    wg_hbm, wu_hbm, wd_hbm, ag_hbm, bg_hbm, au_hbm, bu_hbm, ad_hbm, bd_hbm,
    out_ref, gf_ref, gs_ref, uf_ref, us_ref, df_ref, ds_ref,
    wg_ref, wu_ref, wd_ref, ag_ref, bg_ref, au_ref, bu_ref, ad_ref, bd_ref, w_sem,
    info_ref, zb, stage_same, stage_diff, relay, f_ref,
    p_ref, r1, cpx, xr, back_stage, yr, t_ref, zs, zr, low_ref, rl, ls, rl2, tl,
    info_send, info_recv, swap_sem, ring_send, ring_recv,
    same_send, same_recv, diff_send, diff_recv, x_send, x_recv, core_send, core_recv,
    pc_send, pc_recv, px_send, px_recv, pd_send, pd_recv,
    z_send, z_recv, l_send, l_recv, o_sem,
    out_v, gf_v, gs_v, uf_v, us_v, df_v, ds_v,
):
    xl, xh, y, z, core = place()
    here = functools.partial(device, xl, xh)
    y_others = [here((y + j) % 4, z, core) for j in range(1, 4)]
    x_sides = [device(*side(xl, xh, s), y, z, core) for s in (1, 3)]
    x_far = device(xl, 1 - xh, y, z, core)
    partner = here(y, z, 1 - core)
    down, up = here(y, (z + 7) % 8, core), here(y, (z + 1) % 8, core)

    puts = []

    def put(n, src, dst):
        copy = pltpu.make_async_copy(src, dst, o_sem.at[n])
        copy.start()
        puts.append(copy)

    loads = []
    for n, (src, dst) in enumerate((
        (wg_hbm, wg_ref), (wu_hbm, wu_ref), (wd_hbm, wd_ref), (ag_hbm, ag_ref), (bg_hbm, bg_ref),
        (au_hbm, au_ref), (bu_hbm, bu_ref), (ad_hbm, ad_ref), (bd_hbm, bd_ref),
    )):
        load = pltpu.make_async_copy(src, dst, w_sem.at[n])
        load.start()
        loads.append(load)

    zb[0, 0, :, 0:512] = tok_ref[...]
    zb[0, 0, :, 512:1024] = grad_ref[...]

    ids = ids_ref[...]
    numbers = lax.broadcasted_iota(jnp.int32, (128, 128), 0)
    picked = jnp.zeros((128, 128), F32)
    for k in range(8):
        picked = jnp.where(ids[k : k + 1] == numbers, 1.0, picked)
    later = lax.broadcasted_iota(jnp.int32, (128, 128), 1) > numbers
    before = nn(picked.astype(BF16), jnp.where(later, 1.0, 0.0).astype(BF16))
    for k in range(8):
        slot = jnp.sum(jnp.where(ids[k : k + 1] == numbers, before, 0.0), axis=0, keepdims=True)
        info_ref[0, k : k + 1, :] = ids[k : k + 1].astype(F32) * CAP + slot
    info_ref[0, 8:16, :] = rw_ref[...]

    greet([down, up] + y_others + x_sides + [x_far, partner])

    swap = rem_copy(zb.at[0, 0], zb.at[0, 1], swap_sem.at[0], swap_sem.at[1], x_far)
    swap.start()

    def ring(direction, h, chunk):
        if direction == 0:
            src, dst = (h - 1) % 8, h % 8
        else:
            src, dst = (1 - h) % 8, (-h) % 8
        n = (h - 1) * 2 + chunk
        return rem_copy(
            zb.at[src, chunk], zb.at[dst, chunk],
            ring_send.at[0], ring_recv.at[direction, n],
            down if direction == 0 else up,
        )

    def ring_info(direction, h):
        if direction == 0:
            src, dst = (h - 1) % 8, h % 8
        else:
            src, dst = (1 - h) % 8, (-h) % 8
        return rem_copy(
            info_ref.at[src], info_ref.at[dst],
            info_send.at[0], info_recv.at[direction, h - 1],
            down if direction == 0 else up,
        )

    def advance(h, chunk):
        for direction in (0, 1):
            if chunk == 0 and (h < 4 or direction == 0):
                ring_info(direction, h).wait_recv()
                if h < 3 or (h == 3 and direction == 0):
                    ring_info(direction, h + 1).start()
            if h < 4 or chunk == direction:
                ring(direction, h, chunk).wait_recv()
                if h < 3 or (h == 3 and chunk == direction):
                    ring(direction, h + 1, chunk).start()

    for direction in (0, 1):
        ring_info(direction, 1).start()
        ring(direction, 1, 0).start()
    swap.wait_recv()
    ring(0, 1, 1).start()
    ring(1, 1, 1).start()

    def same_copy(p, e, j, chunk):
        qh = xh if chunk == 0 else 1 - xh
        return rem_copy(
            stage_same.at[p, e, j - 1, chunk], f_ref.at[core, qh, e, p, xl, y],
            same_send.at[0], same_recv.at[p, e],
            here((y + j) % 4, z, core),
        )

    def diff_copy(p, e, j):
        return rem_copy(
            stage_diff.at[p, e, j - 1], relay.at[p, e, y],
            diff_send.at[0], diff_recv.at[p, e], here((y + j) % 4, z, core),
        )

    def x_copy(p, e, s):
        return rem_copy(
            relay.at[p, e], f_ref.at[core, xh, e, p, xl],
            x_send.at[s], x_recv.at[p, e, s], x_sides[s],
        )

    def core_copy(p, e, part):
        if part == 0:
            piece = f_ref.at[core, :, e, p, xl]
        else:
            from_xl, from_xh = side(xl, xh, (1, 3)[part - 1])
            piece = f_ref.at[core, from_xh, e, p, from_xl]
        return rem_copy(piece, piece, core_send.at[part], core_recv.at[p, e, part], partner)

    def pc_copy(p, e):
        return rem_copy(
            p_ref.at[1 - core, :, e, p], r1.at[:, e, p], pc_send.at[0], pc_recv.at[p, e], partner
        )

    def pd_copy(p, e, j):
        return rem_copy(
            back_stage.at[p, e, j - 1], yr.at[p, :, e, y], pd_send.at[0], pd_recv.at[p],
            here((y + j) % 4, z, core),
        )

    def px_copy(p, e, s):
        if s == 2:
            src, dst, to = cpx.at[p, e, 2], xr.at[p, e, 2], x_far
        else:
            _, to_xh = side(xl, xh, (1, 3)[s])
            src, dst, to = cpx.at[p, e, to_xh], xr.at[p, e, xh], x_sides[s]
        return rem_copy(src, dst, px_send.at[0], px_recv.at[p, e], to)

    def z_copy(direction, h, chunk):
        n = direction * 4 + h - 1
        return rem_copy(
            zs.at[n, chunk], zr.at[n, chunk], z_send.at[0], z_recv.at[n, chunk],
            up if direction == 0 else down,
        )

    LOW = (slice(0, 576), slice(576, 768))

    def low_core(n):
        return rem_copy(
            low_ref.at[1 - core, LOW[n]], rl.at[LOW[n]], l_send.at[0, n], l_recv.at[0, n], partner
        )

    def low_far(n):
        return rem_copy(ls.at[LOW[n]], rl2.at[LOW[n]], l_send.at[1, n], l_recv.at[1, n], x_far)

    def low_back(n):
        return rem_copy(
            tl.at[core, LOW[n]], tl.at[core, LOW[n]], l_send.at[2, n], l_recv.at[2, n], partner
        )

    def low_chip(n):
        low_core(n).wait_recv()
        rows = LOW[n]
        ls[rows] = (low_ref[core, rows].astype(F32) + rl[rows].astype(F32)).astype(BF16)
        low_far(n).start()

    def low_total(n):
        low_far(n).wait_recv()
        rows = LOW[n]
        tl[core, rows] = (ls[rows].astype(F32) + rl2[rows].astype(F32)).astype(BF16)
        low_back(n).start()

    table = table_ref[...]

    def row_ids(target_xl, e, first):
        return jnp.concatenate(
            [
                table + ((target_xl * 64 + z * 8 + ((first + j) % 4) * 2 + e) * CAP).astype(F32)
                for j in range(4)
            ],
            axis=0,
        )

    def pair_info(p, weights):
        a, b = PAIRS[p][0] % 8, PAIRS[p][1] % 8
        positions = jnp.concatenate([info_ref[a, 0:8], info_ref[b, 0:8] + FAR], axis=1)
        if not weights:
            return positions, None
        return positions, jnp.concatenate([info_ref[a, 8:16], info_ref[b, 8:16]], axis=1)

    def rows_of(hot, weight, p, chunk):
        a, b = PAIRS[p][0] % 8, PAIRS[p][1] % 8
        rows = nn(hot, jnp.concatenate([zb[a, chunk], zb[b, chunk]], axis=0))
        taken = rows[:, 0:512].astype(BF16)
        scaled = (rows[:, 512:1024] * weight).astype(BF16)
        return jnp.concatenate([taken, scaled], axis=1).reshape(4, 24, 1024)

    def select_diff(p, e):
        hot, weight = one_hot(row_ids(1 - xl, e, y), *pair_info(p, True))
        rows = rows_of(hot, weight, p, 0)
        relay[p, e, y] = rows[0]
        for j in range(1, 4):
            stage_diff[p, e, j - 1] = rows[j]
            diff_copy(p, e, j).start()

    def select_same(p, e, chunks):
        hot, weight = one_hot(row_ids(xl, e, y), *pair_info(p, True))
        for chunk in chunks:
            rows = rows_of(hot, weight, p, chunk)
            f_ref[core, xh if chunk == 0 else 1 - xh, e, p, xl, y] = rows[0]
            for j in range(1, 4):
                stage_same[p, e, j - 1, chunk] = rows[j]
                same_copy(p, e, j, chunk).start()

    def select_a(p):
        for e in (0, 1):
            select_diff(p, e)
        for e in (0, 1):
            select_same(p, e, (0,))

    def select_b(p):
        for e in (0, 1):
            select_same(p, e, (1,))

    def select(p):
        for e in (0, 1):
            select_diff(p, e)
        for e in (0, 1):
            select_same(p, e, (0, 1))

    def forward_x(u):
        p, e = u // 2, u % 2
        drain(stage_diff.at[p, e], diff_recv.at[p, e])
        x_copy(p, e, 0).start()
        x_copy(p, e, 1).start()

    def forward_c(u):
        p, e = u // 2, u % 2
        drain(stage_same.at[p, e], same_recv.at[p, e])
        core_copy(p, e, 0).start()

    def forward(u):
        forward_x(u)
        forward_c(u)

    def gather(u):
        p, e = u // 2, u % 2
        for s in (0, 1):
            x_copy(p, e, 1 - s).wait_recv()
            core_copy(p, e, 1 + s).start()

    def compute(u):
        p, e = u // 2, u % 2
        for part in range(3):
            core_copy(p, e, part).wait_recv()

        def take(cq, qh, lo):
            return f_ref[cq, qh, e, p, :, :, :, lo : lo + 512].reshape(192, 512)

        x = jnp.concatenate([take(0, 0, 0), take(1, 0, 0), take(0, 1, 0), take(1, 1, 0)], axis=1)
        gate_in = jnp.concatenate([wg_ref[e], ag_ref[e]], axis=0)
        up_in = jnp.concatenate([wu_ref[e], au_ref[e]], axis=0)
        down_in = jnp.concatenate([wd_ref[e], bd_ref[e]], axis=0)
        gate = nt(x, gate_in)
        lg = gate[:, 192:256].astype(BF16)
        gate = gate[:, 0:192] + 0.5 * nn(lg, bg_ref[e])
        up_part = nt(x, up_in)
        lu = up_part[:, 192:256].astype(BF16)
        up_part = up_part[:, 0:192] + 0.5 * nn(lu, bu_ref[e])
        sigma = jax.nn.sigmoid(gate)
        active = gate * sigma
        hidden = (active * up_part).astype(BF16)
        down_part = nt(hidden, ad_ref[e]).astype(BF16)
        g = jnp.concatenate(
            [take(0, 0, 512), take(1, 0, 512), take(0, 1, 512), take(1, 1, 512)], axis=1
        )
        gh = nt(g, down_in)
        back = gh[:, 192:256].astype(BF16)
        gh = gh[:, 0:192] + 0.5 * nn(back, ad_ref[e])
        gg = (gh * up_part * sigma * (1.0 + gate * (1.0 - sigma))).astype(BF16)
        gu = (gh * active).astype(BF16)
        gp = nt(gg, bg_ref[e]).astype(BF16)
        upp = nt(gu, bu_ref[e]).astype(BF16)
        left = jnp.concatenate([gg, gp * 0.5], axis=1)
        right = jnp.concatenate([gu, upp * 0.5], axis=1)
        for q in range(4):
            cols = slice(q * 512, q * 512 + 512)
            part = nn(left, gate_in[:, cols]) + nn(right, up_in[:, cols])
            p_ref[q % 2, q // 2, e, p] = part.astype(BF16).reshape(2, 4, 24, 512)
        pc_copy(p, e).start()
        rows = slice(p * 192, p * 192 + 192)
        low_ref[e, rows, 0:64] = down_part
        low_ref[e, rows, 64:128] = gp
        low_ref[e, rows, 128:192] = upp
        for ref, value in ((gs_v, tn(lg, gg)), (us_v, tn(lu, gu)), (df_v, tn(back, hidden))):
            if p == 0:
                ref[e] = 0.5 * value
            else:
                ref[e] += 0.5 * value

    def chip_sum(u):
        p, e = u // 2, u % 2
        pc_copy(p, e).wait_recv()
        for n, qh, xs in ((0, 0, 1 - xl), (1, 1, 1 - xl), (2, 1 - xh, xl)):
            mine = p_ref[core, qh, e, p, xs].astype(F32)
            cpx[p, e, n] = (mine + r1[qh, e, p, xs].astype(F32)).astype(BF16)
        for n in range(3):
            px_copy(p, e, n).start()

    def x_sum(u):
        p, e = u // 2, u % 2
        drain(xr.at[p, e], px_recv.at[p, e])
        for j in range(4):
            to = (y + j) % 4
            same = p_ref[core, xh, e, p, xl, to].astype(F32) + r1[xh, e, p, xl, to].astype(F32)
            same = (same + xr[p, e, 2, to].astype(F32)).astype(BF16)
            diff = (xr[p, e, 0, to].astype(F32) + xr[p, e, 1, to].astype(F32)).astype(BF16)
            if j == 0:
                yr[p, 0, e, y] = same
                yr[p, 1, e, y] = diff
            else:
                back_stage[p, e, j - 1, 0] = same
                back_stage[p, e, j - 1, 1] = diff
                pd_copy(p, e, j).start()

    def combine(p):
        positions, _ = pair_info(p, False)
        hot = jnp.concatenate(
            [
                one_hot(row_ids(target_xl, e, 0), positions, None)
                for target_xl in (xl, 1 - xl)
                for e in (0, 1)
            ],
            axis=0,
        )
        drain(back_stage.at[p], pd_recv.at[p])
        t_ref[p] = tn(hot, yr[p].reshape(384, 512))

    held = {d: (p, i) for p in range(4) for i, d in enumerate(PAIRS[p])}

    def part_of(distance, chunk):
        p, i = held[distance]
        return t_ref[p, i * 128 + chunk * 64 : i * 128 + chunk * 64 + 64]

    def z_hop(direction, h, chunk):
        if h == 1 and chunk != direction:
            return
        n = direction * 4 + h - 1
        distance = 5 - h
        value = part_of(distance if direction == 0 or h == 1 else -distance, chunk)
        if h > 2 or (h == 2 and chunk == direction):
            z_copy(direction, h - 1, chunk).wait_recv()
            value = value + zr[n - 1, chunk].astype(F32)
        zs[n, chunk] = value.astype(BF16)
        z_copy(direction, h, chunk).start()


    def adapters(e):
        quarter = f_ref[core, xh, e].reshape(768, 1024)
        total = tl[e]
        both = 0.5 * tn(total[:, 64:192], quarter[:, 0:512])
        gf_v[e] = both[0:64]
        uf_v[e] = both[64:128]
        ds_v[e] = 0.5 * tn(total[:, 0:64], quarter[:, 512:1024])

    advance(1, 0)
    select_a(0)
    forward_x(0)
    forward_x(1)
    advance(1, 1)
    select_b(0)
    gather(0)
    advance(2, 0)
    select_a(1)
    gather(1)
    forward_c(0)
    forward_c(1)
    for load in loads:
        load.wait()
    compute(0)
    forward_x(2)
    advance(2, 1)
    select_b(1)
    forward_x(3)
    compute(1)
    chip_sum(0)
    advance(3, 0)
    gather(2)
    chip_sum(1)
    forward_c(2)
    advance(3, 1)
    select(2)
    gather(3)
    forward_c(3)
    compute(2)
    forward_x(4)
    x_sum(0)
    advance(4, 0)
    advance(4, 1)
    select(3)
    forward_x(5)
    compute(3)
    gather(4)
    forward_c(4)
    x_sum(1)
    chip_sum(2)
    compute(4)
    gather(5)
    forward_c(5)
    forward_x(6)
    chip_sum(3)
    forward_x(7)
    compute(5)
    x_sum(2)
    gather(6)
    forward_c(6)
    chip_sum(4)
    compute(6)
    gather(7)
    forward_c(7)
    x_sum(3)
    chip_sum(5)
    compute(7)
    low_core(0).start()
    low_core(1).start()
    chip_sum(6)
    x_sum(4)
    chip_sum(7)
    for n, (src, dst) in enumerate(((gs_v, gs_ref), (us_v, us_ref), (df_v, df_ref))):
        put(n, src, dst)
    x_sum(5)
    combine(0)
    combine(1)
    x_sum(6)
    x_sum(7)
    low_chip(0)
    low_chip(1)
    combine(2)
    combine(3)
    z_hop(0, 1, 0)
    z_hop(1, 1, 1)
    for chunk in (1, 0):
        z_hop(0, 2, chunk)
        z_hop(1, 2, chunk)
    drain(zb.at[pl.ds(0, 7)], ring_send.at[0])
    drain(info_ref.at[pl.ds(0, 7)], info_send.at[0])
    swap.wait_send()
    drain(stage_same, same_send.at[0])
    drain(stage_diff, diff_send.at[0])
    drain(relay, x_send.at[0])
    drain(relay, x_send.at[1])
    drain(f_ref.at[0, :, :, :, 0], core_send.at[0])
    drain(f_ref.at[0, 0, :, :, 0], core_send.at[1])
    drain(f_ref.at[0, 0, :, :, 0], core_send.at[2])
    for chunk in (1, 0):
        z_hop(0, 3, chunk)
        z_hop(1, 3, chunk)
    low_total(0)
    low_total(1)
    for chunk in (1, 0):
        z_hop(0, 4, chunk)
        z_hop(1, 4, chunk)
    low_back(0).wait_recv()
    low_back(1).wait_recv()
    adapters(0)
    adapters(1)
    for n, (src, dst) in enumerate(((gf_v, gf_ref), (uf_v, uf_ref), (ds_v, ds_ref))):
        put(n + 3, src, dst)

    def home(chunk):
        z_copy(0, 4, chunk).wait_recv()
        z_copy(1, 4, chunk).wait_recv()
        return part_of(0, chunk) + zr[3, chunk].astype(F32) + zr[7, chunk].astype(F32)

    out_v[64:128] = home(1).astype(BF16)
    out_v[0:64] = home(0).astype(BF16)
    put(6, out_v, out_ref)
    drain(zs.at[pl.ds(0, 7)], z_send.at[0])
    drain(back_stage, pd_send.at[0])
    drain(cpx, px_send.at[0])
    drain(p_ref.at[0], pc_send.at[0])
    for n in (0, 1):
        low_core(n).wait_send()
        low_far(n).wait_send()
        low_back(n).wait_send()
    for copy in puts:
        copy.wait()


def step(tokens, grad_out, ids, weights, table, *frozen):
    vmem = pl.BlockSpec(memory_space=pltpu.VMEM)
    hbm = pl.BlockSpec(memory_space=pl.ANY)
    dma = pltpu.SemaphoreType.DMA

    def buf(*shape):
        return pltpu.VMEM(shape, BF16)

    return pl.pallas_call(
        kernel,
        name="experts",
        out_shape=(
            jax.ShapeDtypeStruct((128, 512), BF16),
            jax.ShapeDtypeStruct((2, 64, 512), F32),
            jax.ShapeDtypeStruct((2, 64, 192), F32),
            jax.ShapeDtypeStruct((2, 64, 512), F32),
            jax.ShapeDtypeStruct((2, 64, 192), F32),
            jax.ShapeDtypeStruct((2, 64, 192), F32),
            jax.ShapeDtypeStruct((2, 64, 512), F32),
        ),
        in_specs=[vmem] * 5 + [hbm] * 9,
        out_specs=(hbm,) * 7,
        scratch_shapes=[buf(*w.shape) for w in frozen] + [
            dma((9,)),
            pltpu.VMEM((8, 16, 128), F32),
            buf(8, 2, 128, 1024),
            buf(4, 2, 3, 2, 24, 1024),
            buf(4, 2, 3, 24, 1024),
            buf(4, 2, 4, 24, 1024),
            buf(2, 2, 2, 4, 2, 4, 24, 1024),
            buf(2, 2, 2, 4, 2, 4, 24, 512),
            buf(2, 2, 4, 2, 4, 24, 512),
            buf(4, 2, 3, 4, 24, 512),
            buf(4, 2, 3, 4, 24, 512),
            buf(4, 2, 3, 2, 24, 512),
            buf(4, 2, 2, 4, 24, 512),
            pltpu.VMEM((4, 256, 512), F32),
            buf(8, 2, 64, 512),
            buf(8, 2, 64, 512),
            buf(2, 768, 192),
            buf(768, 192),
            buf(768, 192),
            buf(768, 192),
            buf(2, 768, 192),
            dma((1,)), dma((2, 4)), dma((2,)), dma((1,)), dma((2, 8)),
            dma((1,)), dma((4, 2)), dma((1,)), dma((4, 2)),
            dma((2,)), dma((4, 2, 2)), dma((3,)), dma((4, 2, 3)),
            dma((1,)), dma((4, 2)), dma((1,)), dma((4, 2)), dma((1,)), dma((4,)),
            dma((1,)), dma((8, 2)), dma((3, 2)), dma((3, 2)), dma((7,)),
            buf(128, 512),
            *[pltpu.VMEM(shape, F32) for shape in (
                (2, 64, 512), (2, 64, 192), (2, 64, 512), (2, 64, 192), (2, 64, 192), (2, 64, 512),
            )],
        ],
        compiler_params=pltpu.CompilerParams(
            collective_id=0, has_side_effects=True, vmem_limit_bytes=VMEM_LIMIT
        ),
    )(tokens, grad_out, ids, weights, table, *frozen)


def finish_kernel(*refs):
    for src, dst in zip(refs[:7], refs[7:]):
        dst[...] = src[...]


def finish(outs):
    vmem = pl.BlockSpec(memory_space=pltpu.VMEM)
    return pl.pallas_call(
        finish_kernel,
        name="finish",
        out_shape=tuple(jax.ShapeDtypeStruct(o.shape, o.dtype) for o in outs),
        in_specs=[vmem] * 7,
        out_specs=(vmem,) * 7,
    )(*outs)


def local(tokens, grad_out, route_weights, expert_ids, wg, wu, wd, ag, bg, au, bu, ad, bd):
    row = np.arange(24)
    table = row % CAP + FAR * (row // CAP)
    table = jnp.asarray(table.reshape(24, 1), F32)
    wg, wu, ag, au, ad = [jnp.swapaxes(w, 1, 2) for w in (wg, wu, ag, au, ad)]
    outs = step(
        tokens, grad_out, expert_ids.T, route_weights.T, table, wg, wu, wd, ag, bg, au, bu, ad, bd
    )
    out, gf, gs, uf, us, df, ds = finish(outs)
    gf, uf, df = [jnp.swapaxes(w, 1, 2) for w in (gf, uf, df)]
    return out, gf, gs, uf, us, df, ds


def solution(mesh):
    specs = (
        P("expert", "tensor"), P("expert", "tensor"), P("expert", None), P("expert", None),
        P("expert", None, "tensor"), P("expert", None, "tensor"), P("expert", "tensor", None),
        P("expert", None, None), P("expert", None, "tensor"), P("expert", None, None),
        P("expert", None, "tensor"), P("expert", "tensor", None), P("expert", None, None),
    )
    outs = (
        P("expert", "tensor"), P("expert", "tensor", None), P("expert", None, "tensor"),
        P("expert", "tensor", None), P("expert", None, "tensor"), P("expert", "tensor", None),
        P("expert", None, "tensor"),
    )
    return jax.shard_map(local, mesh=mesh, in_specs=specs, out_specs=outs, check_vma=False)
```

time: 144 us -> 126 us (0.88)
  Pallas kernels: 141 us -> 123 us
    pallas_call x1, Pallas kernels: 138 us -> 121 us  [step(): pl.pallas_call(kernel, name='experts', out_shape=(jax.ShapeDtypeStruct((1...]
where the time goes in v3:
time: 126 us; the launch traced here: 124 us
  Pallas kernels  123 us (98%)
    pallas_call x1, Pallas kernels, step(): pl.pallas_call(kernel, name='experts', out_shape=(jax.ShapeDtypeStruct((1...  121 us

profile of v3, /device:TPU:24, one launch (start us, length us, event | category | flops | bytes accessed | tf_op | source)
XLA Modules:
  0.0 123.6 jit_solution(12721675031900825131)
XLA Ops:
  0.6 120.6 %experts.1 = (bf16[128,512]{1,0:T(8,128)(2,1)}, f32[2,64,512]{2,1,0:T(8,128)}, f32[2,64,192]{2,1,0:T(8,128)}, f32[2,64,512]{2,1,0:T(8,128)}, f32[2,64,192]{2,1,0...) custom-call(bf16[128,512]{1,0:T(8,128)(2,1)} %tok_ref.1, bf16[128,512]{1,0:T(8,128)(2,1)} %grad_ref.1, ...), custom_call_target="tpu_custom_call" | custom-call | tf_op jit(solution)/shard_map/experts/pallas_call | solution.py:587
  121.3 2.3 %finish.1 = (bf16[128,512]{1,0:T(8,128)(2,1)}, f32[2,64,512]{2,1,0:T(8,128)}, f32[2,64,192]{2,1,0:T(8,128)}, f32[2,64,512]{2,1,0:T(8,128)}, f32[2,64,192]{2,1,0:...) custom-call(bf16[128,512]{1,0:T(8,128)(2,1)} %get-tuple-element.21.refs_0_, ...), custom_call_target="tpu_custom_call" | custom-call | tf_op jit(solution)/shard_map/finish/pallas_call | solution.py:646

commit v4 on v3

--- a/solution.py
+++ b/solution.py
@@ -174,10 +174,6 @@
     for direction in (0, 1):
         ring_info(direction, 1).start()
         ring(direction, 1, 0).start()
-    swap.wait_recv()
-    ring(0, 1, 1).start()
-    ring(1, 1, 1).start()
-
     def same_copy(p, e, j, chunk):
         qh = xh if chunk == 0 else 1 - xh
         return rem_copy(
@@ -301,9 +297,11 @@
                 stage_same[p, e, j - 1, chunk] = rows[j]
                 same_copy(p, e, j, chunk).start()
 
-    def select_a(p):
+    def select_d(p):
         for e in (0, 1):
             select_diff(p, e)
+
+    def select_a(p):
         for e in (0, 1):
             select_same(p, e, (0,))
 
@@ -312,8 +310,6 @@
             select_same(p, e, (1,))
 
     def select(p):
-        for e in (0, 1):
-            select_diff(p, e)
         for e in (0, 1):
             select_same(p, e, (0, 1))
 
@@ -453,81 +449,88 @@
         ds_v[e] = 0.5 * tn(total[:, 0:64], quarter[:, 512:1024])
 
     advance(1, 0)
+    swap.wait_recv()
+    ring(0, 1, 1).start()
+    ring(1, 1, 1).start()
+    select_d(0)
     select_a(0)
     forward_x(0)
     forward_x(1)
+    advance(2, 0)
+    select_d(1)
+    gather(0)
     advance(1, 1)
     select_b(0)
-    gather(0)
-    advance(2, 0)
     select_a(1)
+    forward_x(2)
+    forward_x(3)
     gather(1)
     forward_c(0)
+    advance(3, 0)
+    select_d(2)
     forward_c(1)
     for load in loads:
         load.wait()
     compute(0)
-    forward_x(2)
     advance(2, 1)
     select_b(1)
-    forward_x(3)
+    forward_x(4)
+    gather(2)
+    chip_sum(0)
     compute(1)
-    chip_sum(0)
-    advance(3, 0)
-    gather(2)
+    advance(4, 0)
+    select_d(3)
+    forward_x(5)
+    gather(3)
     chip_sum(1)
     forward_c(2)
     advance(3, 1)
     select(2)
-    gather(3)
     forward_c(3)
     compute(2)
-    forward_x(4)
-    x_sum(0)
-    advance(4, 0)
+    forward_x(6)
+    forward_x(7)
+    gather(4)
     advance(4, 1)
     select(3)
-    forward_x(5)
+    forward_c(4)
     compute(3)
-    gather(4)
-    forward_c(4)
-    x_sum(1)
+    x_sum(0)
     chip_sum(2)
-    compute(4)
     gather(5)
     forward_c(5)
-    forward_x(6)
+    compute(4)
+    x_sum(1)
     chip_sum(3)
-    forward_x(7)
-    compute(5)
-    x_sum(2)
     gather(6)
     forward_c(6)
+    compute(5)
     chip_sum(4)
-    compute(6)
     gather(7)
     forward_c(7)
-    x_sum(3)
-    chip_sum(5)
+    compute(6)
+    x_sum(2)
     compute(7)
     low_core(0).start()
     low_core(1).start()
     chip_sum(6)
-    x_sum(4)
+    x_sum(3)
+    combine(0)
     chip_sum(7)
+    chip_sum(5)
     for n, (src, dst) in enumerate(((gs_v, gs_ref), (us_v, us_ref), (df_v, df_ref))):
         put(n, src, dst)
-    x_sum(5)
-    combine(0)
+    x_sum(4)
     combine(1)
     x_sum(6)
     x_sum(7)
+    combine(3)
+    z_hop(0, 1, 0)
+    z_hop(1, 1, 1)
+    x_sum(5)
     low_chip(0)
     low_chip(1)
     combine(2)
-    combine(3)
-    z_hop(0, 1, 0)
-    z_hop(1, 1, 1)
     for chunk in (1, 0):
         z_hop(0, 2, chunk)
         z_hop(1, 2, chunk)

time: 126 us -> 120 us (0.952); the launches traced: 124 us -> 119 us
  Pallas kernels: 123 us -> 119 us
    pallas_call x1, Pallas kernels: 121 us -> 116 us  [step(): pl.pallas_call(kernel, name='experts', out_shape=(jax.ShapeDtypeStruct((1...]
where the time goes in v4:
time: 120 us; the launch traced here: 119 us
  Pallas kernels  119 us (99%)
    pallas_call x1, Pallas kernels, step(): pl.pallas_call(kernel, name='experts', out_shape=(jax.ShapeDtypeStruct((1...  116 us

profile of v4, /device:TPU:24, one launch (start us, length us, event | category | flops | bytes accessed | tf_op | source)
XLA Modules:
  0.0 119.5 jit_solution(1309816667925344092)
XLA Ops:
  0.6 116.5 %experts.1 = (bf16[128,512]{1,0:T(8,128)(2,1)}, f32[2,64,512]{2,1,0:T(8,128)}, f32[2,64,192]{2,1,0:T(8,128)}, f32[2,64,512]{2,1,0:T(8,128)}, f32[2,64,192]{2,1,0...) custom-call(bf16[128,512]{1,0:T(8,128)(2,1)} %tok_ref.1, bf16[128,512]{1,0:T(8,128)(2,1)} %grad_ref.1, ...), custom_call_target="tpu_custom_call" | custom-call | tf_op jit(solution)/shard_map/experts/pallas_call | solution.py:590
  117.1 2.3 %finish.1 = (bf16[128,512]{1,0:T(8,128)(2,1)}, f32[2,64,512]{2,1,0:T(8,128)}, f32[2,64,192]{2,1,0:T(8,128)}, f32[2,64,512]{2,1,0:T(8,128)}, f32[2,64,192]{2,1,0:...) custom-call(bf16[128,512]{1,0:T(8,128)(2,1)} %get-tuple-element.21.refs_0_, ...), custom_call_target="tpu_custom_call" | custom-call | tf_op jit(solution)/shard_map/finish/pallas_call | solution.py:649

commit v5 on v4

--- a/solution.py
+++ b/solution.py
@@ -52,7 +52,7 @@
     barrier = pltpu.get_barrier_semaphore()
     for target in targets:
         pl.semaphore_signal(barrier, inc=1, device_id=target, device_id_type=MESH)
-    pl.semaphore_wait(barrier, len(targets))
+    return barrier, len(targets)
 
 
 def nt(a, b):
@@ -101,6 +101,7 @@
     partner = here(y, z, 1 - core)
     down, up = here(y, (z + 7) % 8, core), here(y, (z + 1) % 8, core)
 
+    greeted = greet([down, up] + y_others + x_sides + [x_far, partner])
     puts = []
 
     def put(n, src, dst):
@@ -132,7 +133,7 @@
         info_ref[0, k : k + 1, :] = ids[k : k + 1].astype(F32) * CAP + slot
     info_ref[0, 8:16, :] = rw_ref[...]
 
-    greet([down, up] + y_others + x_sides + [x_far, partner])
+    pl.semaphore_wait(*greeted)
 
     swap = rem_copy(zb.at[0, 0], zb.at[0, 1], swap_sem.at[0], swap_sem.at[1], x_far)
     swap.start()

time: 120 us -> 120 us (level)
  no operation moved by 1% of the time
where the time goes in v5:
time: 120 us; the launch traced here: 119 us
  Pallas kernels  119 us (99%)
    pallas_call x1, Pallas kernels, step(): pl.pallas_call(kernel, name='experts', out_shape=(jax.ShapeDtypeStruct((1...  116 us

profile of v5, /device:TPU:24, one launch (start us, length us, event | category | flops | bytes accessed | tf_op | source)
XLA Modules:
  0.0 119.3 jit_solution(3634798202149061443)
XLA Ops:
  0.6 116.3 %experts.1 = (bf16[128,512]{1,0:T(8,128)(2,1)}, f32[2,64,512]{2,1,0:T(8,128)}, f32[2,64,192]{2,1,0:T(8,128)}, f32[2,64,512]{2,1,0:T(8,128)}, f32[2,64,192]{2,1,0...) custom-call(bf16[128,512]{1,0:T(8,128)(2,1)} %tok_ref.1, bf16[128,512]{1,0:T(8,128)(2,1)} %grad_ref.1, ...), custom_call_target="tpu_custom_call" | custom-call | tf_op jit(solution)/shard_map/experts/pallas_call | solution.py:591
  116.9 2.3 %finish.1 = (bf16[128,512]{1,0:T(8,128)(2,1)}, f32[2,64,512]{2,1,0:T(8,128)}, f32[2,64,192]{2,1,0:T(8,128)}, f32[2,64,512]{2,1,0:T(8,128)}, f32[2,64,192]{2,1,0:...) custom-call(bf16[128,512]{1,0:T(8,128)(2,1)} %get-tuple-element.21.refs_0_, ...), custom_call_target="tpu_custom_call" | custom-call | tf_op jit(solution)/shard_map/finish/pallas_call | solution.py:650
